TPU v7x, 32 devices: a whole 2x2x4 slice. The times are simulated.
32 devices in a mesh: section: 2 (over y), pen: 8 (over z, x), slab: 2 (over core).
Axes of the slice: x: 2, y: 2, z: 4, core: 2. Of those that a mesh axis runs over, the one named last changes fastest.
Arguments:
- velocity: float32 [3, 48, 48, 48], P(None, ('section', 'pen'), 'slab'), may hold values from -6 to 6
- vorticity: float32 [3, 48, 48, 48], P(None, ('section', 'pen'), 'slab'), may hold values from -6 to 6
- velocity_modes: float32 [3, 32, 32, 2, 32], P(None, None, ('section', 'pen'), None, 'slab'), may hold values from -6 to 6
Outputs:
- rhs_modes: float32 [3, 32, 32, 2, 32], P(None, None, ('section', 'pen'), None, 'slab')
All inputs are finite; a program needn't handle non-finite values.
Results may differ from a plain program's by a relative error of at most 0.000057.
Values sent between devices are 32-bit elements; how exact they have to be, the bound alone decides.
A program may use at most 64 MiB of HBM per device.

v0:
```python
import functools
import math

import jax
import jax.numpy as jnp
import numpy as np
from jax import lax
from jax.experimental import pallas as pl
from jax.experimental.pallas import tpu as pltpu
from jax.sharding import PartitionSpec as P

AXES = ("section", "pen", "slab")
highest = lax.Precision.HIGHEST


def signed_modes(index, count):
    return jnp.where(index < count // 2, index, index - count)


def discrete_fourier_tables(length, keep_count):
    modes = signed_modes(jnp.arange(keep_count, dtype=jnp.int32), keep_count)
    mode_positions = jnp.arange(length, dtype=jnp.int32)
    phase = jnp.remainder(modes[:, None] * mode_positions[None, :], length).astype(jnp.float32)
    angles = 2.0 * math.pi / length * phase
    factor = 1.0 / math.sqrt(length)
    return (jnp.cos(angles) * factor, jnp.sin(angles) * factor)


def complex_apply(form, cosine, sine, real_part, imag_part):
    out_real = jnp.einsum(form, cosine, real_part, precision=highest) + jnp.einsum(
        form, sine, imag_part, precision=highest
    )
    out_imag = jnp.einsum(form, cosine, imag_part, precision=highest) - jnp.einsum(
        form, sine, real_part, precision=highest
    )
    return (out_real, out_imag)


def per_device(velocity, vorticity, velocity_modes):
    grid_cells = velocity.shape[3]
    keep_count = velocity_modes.shape[1]
    cross_product = jnp.stack(
        [
            velocity[1] * vorticity[2] - velocity[2] * vorticity[1],
            velocity[2] * vorticity[0] - velocity[0] * vorticity[2],
            velocity[0] * vorticity[1] - velocity[1] * vorticity[0],
        ]
    )
    slabs = lax.axis_size("slab")
    block_modes = keep_count // slabs
    cosine_table, sine_table = discrete_fourier_tables(grid_cells, keep_count)
    cols_real = cosine_table.T.reshape(grid_cells, slabs, block_modes)
    cols_imag = (-sine_table).T.reshape(grid_cells, slabs, block_modes)
    column_table = jnp.stack([cols_real, cols_imag], axis=2).reshape(grid_cells, 2 * keep_count)
    first_pass = jnp.einsum("czyx,xj->czyj", cross_product, column_table, precision=highest)
    block = lax.all_to_all(first_pass, "slab", split_axis=3, concat_axis=2, tiled=True)
    out_real, out_imag = complex_apply(
        "ky,czyj->czkj",
        cosine_table,
        sine_table,
        block[..., :block_modes],
        block[..., block_modes:],
    )
    second_pass = jnp.concatenate([out_real, out_imag], axis=-1)
    halves = lax.axis_size("section")
    pens = lax.axis_size("pen")
    rows_ky = keep_count // (halves * pens)
    block = lax.all_to_all(second_pass, ("section", "pen"), split_axis=2, concat_axis=1, tiled=True)
    out_real, out_imag = complex_apply(
        "kz,czyj->ckyj",
        cosine_table,
        sine_table,
        block[..., :block_modes],
        block[..., block_modes:],
    )
    third_pass = jnp.concatenate([out_real, out_imag], axis=-1)
    group_index = lax.axis_index("section") * pens + lax.axis_index("pen")
    modes_z = signed_modes(jnp.arange(keep_count, dtype=jnp.int32), keep_count)[:, None, None]
    modes_y = signed_modes(
        group_index * rows_ky + jnp.arange(rows_ky, dtype=jnp.int32), keep_count
    )[None, :, None]
    modes_x = signed_modes(
        lax.axis_index("slab") * block_modes + jnp.arange(block_modes, dtype=jnp.int32), keep_count
    )[None, None, :]
    limit = -(keep_count // 2)
    keep_mask = ((modes_x != limit) & (modes_y != limit) & (modes_z != limit)).astype(jnp.float32)
    waves = (modes_x.astype(jnp.float32), modes_y.astype(jnp.float32), modes_z.astype(jnp.float32))
    ksq = waves[0] * waves[0] + waves[1] * waves[1] + waves[2] * waves[2]
    denom = jnp.maximum(ksq, 1.0)
    parts = []
    for which in range(2):
        chosen = third_pass[..., which * block_modes : (which + 1) * block_modes]
        comp = [chosen[c] for c in range(3)]
        inner = (waves[0] * comp[0] + waves[1] * comp[1] + waves[2] * comp[2]) / denom
        parts.append(jnp.stack([comp[c] - waves[c] * inner for c in range(3)]))
    projected = jnp.stack(parts, axis=3)
    visc = 0.5 / (keep_count // 2) ** 2
    return (
        projected * keep_mask[None, :, :, None, :]
        - visc * ksq[None, :, :, None, :] * velocity_modes
    )


def split_bf16(table):
    high = table.astype(jnp.bfloat16)
    low = (table - high.astype(np.float32)).astype(jnp.bfloat16)
    return high, low


def split_in_kernel(value):
    high = value.astype(jnp.bfloat16)
    low = (value - high.astype(jnp.float32)).astype(jnp.bfloat16)
    return high, low


def mm(a, b):
    return lax.dot_general(a, b, (((1,), (0,)), ((), ())), preferred_element_type=jnp.float32)


def split_dot(a, b):
    return mm(a[0], b[0]) + mm(a[1], b[0]) + mm(a[0], b[1])


def wave_numbers(count):
    index = np.arange(count)
    return np.where(index < count // 2, index, index - count)


def host_tables(cells, keep):
    phase = np.remainder(wave_numbers(keep)[:, None] * np.arange(cells)[None, :], cells)
    angles = 2.0 * np.pi / cells * phase
    factor = 1.0 / np.sqrt(cells)
    return np.cos(angles) * factor, np.sin(angles) * factor


class Plan:
    def __init__(self, mesh_shape, cells, keep, z_rows, y_rows):
        self.cells, self.keep, self.z_rows, self.y_rows = cells, keep, z_rows, y_rows
        self.halves, self.pens, self.slabs = (mesh_shape[a] for a in AXES)
        self.groups = self.halves * self.pens
        self.count = self.groups * self.slabs
        self.rows_ky = keep // self.groups
        self.block = keep // self.slabs
        self.field = self.rows_ky * 2 * self.block
        self.rows = z_rows + (z_rows + 1) // 2
        self.slots = 2 * self.rows_ky

    def fits(self):
        return (
            2 * self.field == 128
            and self.rows <= 8
            and (self.rows * self.groups) % 16 == 0
            and self.y_rows % 8 == 0
            and self.keep % 8 == 0
            and self.block % 8 == 0
            and 3 * self.z_rows * self.y_rows <= 512
            and self.count <= 64
        )

    def place(self, comp, z):
        if comp < 2:
            return z, comp
        return self.z_rows + z // 2, z % 2

    def tables(self):
        cos, sin = host_tables(self.cells, self.keep)
        g, zl, yl, ky_n, bm = self.groups, self.z_rows, self.y_rows, self.rows_ky, self.block
        first = np.zeros((self.slabs, self.slots, 2, self.rows, g, 3, zl, yl), np.float32)
        for c in range(3):
            for z in range(zl):
                row, half = self.place(c, z)
                for ky in range(ky_n):
                    for s in range(self.slabs):
                        cells = slice(s * yl, (s + 1) * yl)
                        first[s, half * ky_n + ky, 0, row, :, c, z] = cos[ky::ky_n, cells]
                        first[s, half * ky_n + ky, 1, row, :, c, z] = -sin[ky::ky_n, cells]
        first = first.reshape(self.slabs, self.slots * 2 * self.rows * g, 3 * zl * yl)
        second = np.zeros((self.slots, 2, self.cells, self.slabs, self.slots, 2, bm), np.float32)
        for s in range(self.slabs):
            c_t = cos[s * bm : (s + 1) * bm].T
            s_t = sin[s * bm : (s + 1) * bm].T
            for q in range(self.slots):
                second[q, 0, :, s, q, 0] = c_t
                second[q, 0, :, s, q, 1] = -s_t
                second[q, 1, :, s, q, 0] = s_t
                second[q, 1, :, s, q, 1] = c_t
        second = second.reshape(self.slots, 2 * self.cells, self.slabs * 128)
        third = np.zeros((3, 2, self.keep, g, self.slabs, 8), np.float32)
        for z in range(zl):
            for which, table in enumerate((cos, sin)):
                column = table[:, z::zl][:, :, None]
                third[0, which, :, :, :, z] = column
                third[1 + z % 2, which, :, :, :, zl + z // 2] = column
        third = third.reshape(6 * self.keep, self.count * 8)
        return (
            np.stack(split_bf16(first), axis=1),
            np.stack(split_bf16(second)),
            np.stack(split_bf16(third)),
        )


def kernel(
    plan, vel_hbm, vort_hbm, modes_hbm, first_hbm, second_hbm, third_hbm, out_ref,
    vel, vort, modes, first, second, third, send, recv, load_sem, send_sem, recv_sem,
):
    sec, pen, slab = (lax.axis_index(a) for a in AXES)
    group = sec * plan.pens + pen
    me = group * plan.slabs + slab
    loads = [
        pltpu.make_async_copy(src, dst, load_sem.at[i])
        for i, (src, dst) in enumerate(
            (
                (vel_hbm, vel),
                (vort_hbm, vort),
                (first_hbm.at[slab], first),
                (second_hbm, second),
                (third_hbm, third),
                (modes_hbm, modes),
            )
        )
    ]
    for load in loads:
        load.start()

    def spread(offset):
        a, b, c = offset
        to = (
            lax.rem(sec + a, plan.halves),
            lax.rem(pen + b, plan.pens),
            lax.rem(slab + c, plan.slabs),
        )
        back = (
            lax.rem(sec + plan.halves - a, plan.halves),
            lax.rem(pen + plan.pens - b, plan.pens),
            lax.rem(slab + plan.slabs - c, plan.slabs),
        )
        return to, (back[0] * plan.pens + back[1]) * plan.slabs + back[2]

    offsets = [
        (a, b, c)
        for b in sorted(range(plan.pens), key=lambda v: -min(v, plan.pens - v))
        for a in reversed(range(plan.halves))
        for c in reversed(range(plan.slabs))
    ]
    offsets.remove((0, 0, 0))
    recv[...] = jnp.zeros_like(recv)
    barrier = pltpu.get_barrier_semaphore()
    for offset in offsets:
        pl.semaphore_signal(
            barrier, inc=1, device_id=spread(offset)[0], device_id_type=pl.DeviceIdType.MESH
        )

    loads[0].wait()
    loads[1].wait()
    zl, yl, cells = plan.z_rows, plan.y_rows, plan.cells
    v = [vel[c].reshape(zl * yl, cells) for c in range(3)]
    w = [vort[c].reshape(zl * yl, cells) for c in range(3)]
    cross = jnp.concatenate(
        [v[1] * w[2] - v[2] * w[1], v[2] * w[0] - v[0] * w[2], v[0] * w[1] - v[1] * w[0]], axis=0
    )
    cross = split_in_kernel(cross)
    loads[2].wait()
    part = split_dot((first[0], first[1]), cross)
    loads[3].wait()
    size = plan.rows * plan.groups
    total = None
    for i in range(plan.slots):
        halves = [part[j * size : (j + 1) * size] for j in (2 * i, 2 * i + 1)]
        piece = split_in_kernel(jnp.concatenate(halves, axis=1))
        term = split_dot(piece, (second[0, i], second[1, i]))
        total = term if total is None else total + term
    for s in range(plan.slabs):
        for r in range(plan.rows):
            send[s, :, r, :] = total[r * plan.groups : (r + 1) * plan.groups, s * 128 : (s + 1) * 128]

    pl.semaphore_wait(barrier, plan.count - 1)
    used = pl.ds(0, plan.rows)
    copies = []
    for i, offset in enumerate(offsets):
        to, source = spread(offset)
        copy = pltpu.make_async_remote_copy(
            src_ref=send.at[to[2], to[0] * plan.pens + to[1], used],
            dst_ref=recv.at[me, used],
            send_sem=send_sem.at[i],
            recv_sem=recv_sem.at[i],
            device_id=to,
            device_id_type=pl.DeviceIdType.MESH,
        )
        copy.start()
        arrival = pltpu.make_async_remote_copy(
            src_ref=send.at[to[2], to[0] * plan.pens + to[1], used],
            dst_ref=recv.at[source, used],
            send_sem=send_sem.at[i],
            recv_sem=recv_sem.at[i],
            device_id=to,
            device_id_type=pl.DeviceIdType.MESH,
        )
        copies.append((copy, arrival))
    recv[me, 0 : plan.rows] = send[slab, group, 0 : plan.rows]

    keep, bm, ky_n = plan.keep, plan.block, plan.rows_ky

    def signed(index):
        return jnp.where(index < keep // 2, index, index - keep)

    lane = lax.broadcasted_iota(jnp.int32, (keep, 128), 1)
    inner_lane = lax.rem(lane, plan.field)
    low_half = lane < plan.field
    is_real = lax.rem(lane // bm, 2) == 0
    kx = signed(lax.rem(lane, bm) + slab * bm)
    ky = signed(inner_lane // (2 * bm) + group * ky_n)
    kz = signed(lax.broadcasted_iota(jnp.int32, (keep, 128), 0))
    limit = -(keep // 2)
    mask = ((kx != limit) & (ky != limit) & (kz != limit)).astype(jnp.float32)
    kx, ky, kz = (k.astype(jnp.float32) for k in (kx, ky, kz))
    inverse = 1.0 / jnp.maximum(kx * kx + ky * ky + kz * kz, 1.0)
    pair = jnp.where(low_half, kx, ky)

    row = lax.broadcasted_iota(jnp.int32, (plan.field, keep), 0)
    kz_t = signed(lax.broadcasted_iota(jnp.int32, (plan.field, keep), 1)).astype(jnp.float32)
    kx_t = signed(lax.rem(row, bm) + slab * bm).astype(jnp.float32)
    ky_t = signed(row // (2 * bm) + group * ky_n).astype(jnp.float32)
    visc = 0.5 / (keep // 2) ** 2
    damp = visc * (kx_t * kx_t + ky_t * ky_t + kz_t * kz_t)
    loads[5].wait()
    damped = [damp * modes[c].reshape(plan.field, keep) for c in range(3)]
    loads[4].wait()

    for _, arrival in copies:
        arrival.wait_recv()
    got = split_in_kernel(recv[...].reshape(plan.count * 8, 128))
    out = split_dot((third[0], third[1]), got)
    out = [out[i * keep : (i + 1) * keep] for i in range(6)]

    def turn(cos_part, sin_part):
        ahead = pltpu.roll(sin_part, 128 - bm, 1)
        behind = pltpu.roll(sin_part, bm, 1)
        return cos_part + jnp.where(is_real, ahead, -behind)

    both = turn(out[0], out[1])
    last_cos = jnp.where(low_half, out[2], out[4])
    last_sin = jnp.where(low_half, out[3], out[5])
    last = turn(last_cos, last_sin)
    last = last + pltpu.roll(last, plan.field, 1)
    dots = pair * both
    inner = (dots + pltpu.roll(dots, plan.field, 1) + kz * last) * inverse
    both = jnp.transpose((both - pair * inner) * mask)
    last = jnp.transpose((last - kz * inner) * mask)
    shape = (ky_n, 2, bm, keep)
    out_ref[0] = (both[: plan.field] - damped[0]).reshape(shape)
    out_ref[1] = (both[plan.field :] - damped[1]).reshape(shape)
    out_ref[2] = (last[: plan.field] - damped[2]).reshape(shape)
    for copy, _ in copies:
        copy.wait_send()


def direct(plan, tables, velocity, vorticity, velocity_modes):
    modes = jnp.transpose(velocity_modes, (0, 2, 3, 4, 1))
    first, second, third = tables
    hbm = pl.BlockSpec(memory_space=pltpu.HBM)
    out = pl.pallas_call(
        functools.partial(kernel, plan),
        out_shape=pltpu.VMEM(modes.shape, jnp.float32),
        in_specs=[hbm] * 6,
        out_specs=pl.BlockSpec(memory_space=pltpu.VMEM),
        scratch_shapes=[
            pltpu.VMEM(velocity.shape, jnp.float32),
            pltpu.VMEM(vorticity.shape, jnp.float32),
            pltpu.VMEM(modes.shape, jnp.float32),
            pltpu.VMEM(first.shape[1:], jnp.bfloat16),
            pltpu.VMEM(second.shape, jnp.bfloat16),
            pltpu.VMEM(third.shape, jnp.bfloat16),
            pltpu.VMEM((plan.slabs, plan.groups, 8, 128), jnp.float32),
            pltpu.VMEM((plan.count, 8, 128), jnp.float32),
            pltpu.SemaphoreType.DMA((6,)),
            pltpu.SemaphoreType.DMA((plan.count - 1,)),
            pltpu.SemaphoreType.DMA((plan.count - 1,)),
        ],
        compiler_params=pltpu.CompilerParams(collective_id=0, has_side_effects=True),
    )(velocity, vorticity, modes, first, second, third)
    return jnp.transpose(out, (0, 4, 1, 2, 3))


def solution(mesh):
    sizes = dict(mesh.shape)

    def run(velocity, vorticity, velocity_modes):
        _, z_rows, y_rows, cells = velocity.shape
        plan = Plan(sizes, cells, velocity_modes.shape[1], z_rows, y_rows)
        if not plan.fits():
            return per_device(velocity, vorticity, velocity_modes)
        return direct(plan, plan.tables(), velocity, vorticity, velocity_modes)

    return jax.shard_map(
        run,
        mesh=mesh,
        in_specs=(
            P(None, ("section", "pen"), "slab", None),
            P(None, ("section", "pen"), "slab", None),
            P(None, None, ("section", "pen"), None, "slab"),
        ),
        out_specs=P(None, None, ("section", "pen"), None, "slab"),
        check_vma=False,
    )
```

profile of v0, /device:TPU:0, one launch (start us, length us, event | category | flops | bytes accessed | tf_op | source)
XLA Modules:
  0.0 13.2 jit_solution(2952458714775515034)
XLA Ops:
  0.0 12.6 %shard_map.64 = f32[3,2,2,16,32]{4,3,2,1,0:T(8,128)S(1)} custom-call(f32[3,3,24,48]{3,2,1,0:T(8,128)} %vel_hbm.1, f32[3,3,24,48]{3,2,1,0:T(8,128)} %vort_hbm.1, f32[3,2,2,16,32]{4,3,2,1,0:T(8,128)} %bitcast.3, bf16[2,2,640,216]{3,2,1,0:T(8,128)(2,1)} %constant.6.clone.first_hbm, bf16[2,4,96,256]{3,2,1,0:T(8,128)(2,1)} %constant.7.clone.second_hbm, ...), custom_call_target="tpu_custom_call" | custom-call | tf_op jit(solution)/shard_map/pallas_call | solution.py:361
  12.6 0.6 %copy.8 = f32[3,32,2,2,16]{1,4,3,2,0:T(8,128)} copy(f32[3,32,2,2,16]{1,4,3,2,0:T(8,128)S(1)} %bitcast.2) | data formatting | bytes 49152
where the time goes:
time: 13.4 us; the launch traced here: 13.2 us
  Pallas kernels  12.6 us (94%)
  local copies, waits for them, and re-layouts  0.64 us (5%)
    pallas_call x1, Pallas kernels, direct(): pl.pallas_call(functools.partial(kernel, plan), out_shape=pltpu.VMEM(mode...  12.6 us
    unnamed x1, local copies, waits for them, and re-layouts  0.64 us

commit v1 on v0

v1 whole, which is shorter than its diff:
```python
import functools
import math

import jax
import jax.numpy as jnp
import numpy as np
from jax import lax
from jax.experimental import pallas as pl
from jax.experimental.pallas import tpu as pltpu
from jax.sharding import PartitionSpec as P

AXES = ("section", "pen", "slab")
highest = lax.Precision.HIGHEST


def signed_modes(index, count):
    return jnp.where(index < count // 2, index, index - count)


def discrete_fourier_tables(length, keep_count):
    modes = signed_modes(jnp.arange(keep_count, dtype=jnp.int32), keep_count)
    mode_positions = jnp.arange(length, dtype=jnp.int32)
    phase = jnp.remainder(modes[:, None] * mode_positions[None, :], length).astype(jnp.float32)
    angles = 2.0 * math.pi / length * phase
    factor = 1.0 / math.sqrt(length)
    return (jnp.cos(angles) * factor, jnp.sin(angles) * factor)


def complex_apply(form, cosine, sine, real_part, imag_part):
    out_real = jnp.einsum(form, cosine, real_part, precision=highest) + jnp.einsum(
        form, sine, imag_part, precision=highest
    )
    out_imag = jnp.einsum(form, cosine, imag_part, precision=highest) - jnp.einsum(
        form, sine, real_part, precision=highest
    )
    return (out_real, out_imag)


def per_device(velocity, vorticity, velocity_modes):
    grid_cells = velocity.shape[3]
    keep_count = velocity_modes.shape[1]
    cross_product = jnp.stack(
        [
            velocity[1] * vorticity[2] - velocity[2] * vorticity[1],
            velocity[2] * vorticity[0] - velocity[0] * vorticity[2],
            velocity[0] * vorticity[1] - velocity[1] * vorticity[0],
        ]
    )
    slabs = lax.axis_size("slab")
    block_modes = keep_count // slabs
    cosine_table, sine_table = discrete_fourier_tables(grid_cells, keep_count)
    cols_real = cosine_table.T.reshape(grid_cells, slabs, block_modes)
    cols_imag = (-sine_table).T.reshape(grid_cells, slabs, block_modes)
    column_table = jnp.stack([cols_real, cols_imag], axis=2).reshape(grid_cells, 2 * keep_count)
    first_pass = jnp.einsum("czyx,xj->czyj", cross_product, column_table, precision=highest)
    block = lax.all_to_all(first_pass, "slab", split_axis=3, concat_axis=2, tiled=True)
    out_real, out_imag = complex_apply(
        "ky,czyj->czkj",
        cosine_table,
        sine_table,
        block[..., :block_modes],
        block[..., block_modes:],
    )
    second_pass = jnp.concatenate([out_real, out_imag], axis=-1)
    halves = lax.axis_size("section")
    pens = lax.axis_size("pen")
    rows_ky = keep_count // (halves * pens)
    block = lax.all_to_all(second_pass, ("section", "pen"), split_axis=2, concat_axis=1, tiled=True)
    out_real, out_imag = complex_apply(
        "kz,czyj->ckyj",
        cosine_table,
        sine_table,
        block[..., :block_modes],
        block[..., block_modes:],
    )
    third_pass = jnp.concatenate([out_real, out_imag], axis=-1)
    group_index = lax.axis_index("section") * pens + lax.axis_index("pen")
    modes_z = signed_modes(jnp.arange(keep_count, dtype=jnp.int32), keep_count)[:, None, None]
    modes_y = signed_modes(
        group_index * rows_ky + jnp.arange(rows_ky, dtype=jnp.int32), keep_count
    )[None, :, None]
    modes_x = signed_modes(
        lax.axis_index("slab") * block_modes + jnp.arange(block_modes, dtype=jnp.int32), keep_count
    )[None, None, :]
    limit = -(keep_count // 2)
    keep_mask = ((modes_x != limit) & (modes_y != limit) & (modes_z != limit)).astype(jnp.float32)
    waves = (modes_x.astype(jnp.float32), modes_y.astype(jnp.float32), modes_z.astype(jnp.float32))
    ksq = waves[0] * waves[0] + waves[1] * waves[1] + waves[2] * waves[2]
    denom = jnp.maximum(ksq, 1.0)
    parts = []
    for which in range(2):
        chosen = third_pass[..., which * block_modes : (which + 1) * block_modes]
        comp = [chosen[c] for c in range(3)]
        inner = (waves[0] * comp[0] + waves[1] * comp[1] + waves[2] * comp[2]) / denom
        parts.append(jnp.stack([comp[c] - waves[c] * inner for c in range(3)]))
    projected = jnp.stack(parts, axis=3)
    visc = 0.5 / (keep_count // 2) ** 2
    return (
        projected * keep_mask[None, :, :, None, :]
        - visc * ksq[None, :, :, None, :] * velocity_modes
    )


def split_bf16(table):
    high = table.astype(jnp.bfloat16)
    low = (table - high.astype(np.float32)).astype(jnp.bfloat16)
    return high, low


def split_in_kernel(value):
    high = value.astype(jnp.bfloat16)
    low = (value - high.astype(jnp.float32)).astype(jnp.bfloat16)
    return high, low


def mm(a, b):
    return lax.dot_general(a, b, (((1,), (0,)), ((), ())), preferred_element_type=jnp.float32)


def split_dot(a, b):
    return mm(a[0], b[0]) + mm(a[1], b[0]) + mm(a[0], b[1])


def wave_numbers(count):
    index = np.arange(count)
    return np.where(index < count // 2, index, index - count)


def host_tables(cells, keep):
    phase = np.remainder(wave_numbers(keep)[:, None] * np.arange(cells)[None, :], cells)
    angles = 2.0 * np.pi / cells * phase
    factor = 1.0 / np.sqrt(cells)
    return np.cos(angles) * factor, np.sin(angles) * factor


class Plan:
    def __init__(self, mesh_shape, cells, keep, z_rows, y_rows):
        self.cells, self.keep, self.z_rows, self.y_rows = cells, keep, z_rows, y_rows
        self.halves, self.pens, self.slabs = (mesh_shape[a] for a in AXES)
        self.groups = self.halves * self.pens
        self.count = self.groups * self.slabs
        self.rows_ky = keep // self.groups
        self.block = keep // self.slabs
        self.width = self.rows_ky * self.block
        self.rows = 2 * z_rows
        self.wide = self.slabs * 128

    def fits(self):
        return (
            self.rows_ky * self.groups == self.keep
            and self.block * self.slabs == self.keep
            and 3 * self.width <= 128
            and 128 % self.width == 0
            and self.rows <= 8
            and self.cells <= 128
            and self.cells % 16 == 0
            and self.y_rows % 8 == 0
            and 6 * self.y_rows <= 256
            and self.groups % 8 == 0
            and self.keep % 8 == 0
            and self.block % 8 == 0
            and 3 * self.z_rows * self.y_rows <= 512
            and 2 <= self.count <= 64
        )

    def tables(self):
        cos, sin = host_tables(self.cells, self.keep)
        g, zl, yl, ky_n, bm = self.groups, self.z_rows, self.y_rows, self.rows_ky, self.block
        first = np.zeros((self.cells, 2, self.slabs, 128 // self.width, ky_n, bm), np.float32)
        for s in range(self.slabs):
            modes = slice(s * bm, (s + 1) * bm)
            first[:, 0, s, :3] = cos[modes].T[:, None, None]
            first[:, 1, s, :3] = -sin[modes].T[:, None, None]
        first = first.reshape(self.cells, 2 * self.wide)
        second = np.zeros((self.slabs, 2, ky_n, g, 2, yl), np.float32)
        for s in range(self.slabs):
            for k in range(ky_n):
                c = cos[k::ky_n, s * yl : (s + 1) * yl]
                n = sin[k::ky_n, s * yl : (s + 1) * yl]
                second[s, 0, k, :, 0], second[s, 0, k, :, 1] = c, n
                second[s, 1, k, :, 0], second[s, 1, k, :, 1] = -n, c
        second = second.reshape(self.slabs, 2 * self.keep, 2 * yl)
        third = np.zeros((2, self.keep, g, self.slabs, 8), np.float32)
        for z in range(zl):
            c, n = cos[:, z::zl][:, :, None], sin[:, z::zl][:, :, None]
            third[0, :, :, :, 2 * z], third[0, :, :, :, 2 * z + 1] = c, n
            third[1, :, :, :, 2 * z], third[1, :, :, :, 2 * z + 1] = -n, c
        third = third.reshape(2 * self.keep, self.count * 8)
        high, low = split_bf16(second)
        return (
            np.stack(split_bf16(first)),
            np.concatenate([high, high, low], axis=2),
            np.stack(split_bf16(third)),
        )


def kernel(
    plan, vel_hbm, vort_hbm, modes_hbm, first_hbm, second_hbm, third_hbm, out_ref,
    fields, modes, first, second, third, cross, send, recv,
    field_sem, table_sem, late_sem, send_sem, recv_sem,
):
    sec, pen, slab = (lax.axis_index(a) for a in AXES)
    group = sec * plan.pens + pen
    me = group * plan.slabs + slab
    cells, keep = plan.cells, plan.keep
    for i, source in enumerate((vel_hbm, vort_hbm)):
        for c in range(3):
            pltpu.make_async_copy(source.at[c], fields.at[i, c], field_sem).start()
    table_loads = [
        pltpu.make_async_copy(first_hbm.at[0], first.at[0, 0:cells], table_sem.at[0]),
        pltpu.make_async_copy(first_hbm.at[0], first.at[1, 0:cells], table_sem.at[1]),
        pltpu.make_async_copy(first_hbm.at[1], first.at[2, 0:cells], table_sem.at[2]),
        pltpu.make_async_copy(second_hbm.at[slab], second, table_sem.at[3]),
    ]
    late_loads = [
        pltpu.make_async_copy(third_hbm, third, late_sem.at[0]),
        pltpu.make_async_copy(modes_hbm, modes, late_sem.at[1]),
    ]
    for load in table_loads + late_loads:
        load.start()

    def spread(offset):
        a, b, c = offset
        return (
            lax.rem(sec + a, plan.halves),
            lax.rem(pen + b, plan.pens),
            lax.rem(slab + c, plan.slabs),
        )

    offsets = [
        (a, b, c)
        for b in sorted(range(plan.pens), key=lambda v: -min(v, plan.pens - v))
        for a in reversed(range(plan.halves))
        for c in reversed(range(plan.slabs))
    ]
    offsets.remove((0, 0, 0))
    barrier = pltpu.get_barrier_semaphore()
    for offset in offsets:
        pl.semaphore_signal(
            barrier, inc=1, device_id=spread(offset), device_id_type=pl.DeviceIdType.MESH
        )
    if plan.rows < 8:
        recv[:, plan.rows : 8] = jnp.zeros((plan.count, 8 - plan.rows, 128), jnp.float32)
    cross[...] = jnp.zeros_like(cross)
    if cells < 128:
        for i in range(3):
            first[i, cells:128] = jnp.zeros((128 - cells, first.shape[2]), jnp.bfloat16)

    pltpu.make_async_copy(fields, fields, field_sem).wait()
    zl, yl = plan.z_rows, plan.y_rows
    area = zl * yl
    v, w = ([fields[i, c].reshape(area, cells) for c in range(3)] for i in range(2))
    for c in range(3):
        p, q = (c + 1) % 3, (c + 2) % 3
        cross[c * area : (c + 1) * area, 0:cells] = v[p] * w[q] - v[q] * w[p]
    for load in table_loads:
        load.wait()
    high, low = split_in_kernel(cross[...])
    along_x = mm(
        jnp.concatenate([high, low], axis=1), jnp.concatenate([first[0], first[1]], axis=0)
    ) + mm(high, first[2])
    slot = lax.broadcasted_iota(jnp.int32, (area, 2 * plan.wide), 1) % 128 // plan.width
    along_x = [along_x[c * area : (c + 1) * area] for c in range(3)]
    along_x = jnp.where(slot == 0, along_x[0], jnp.where(slot == 1, along_x[1], along_x[2]))
    high = along_x.astype(jnp.bfloat16).astype(jnp.float32)
    low = along_x - high
    upper = lax.broadcasted_iota(jnp.int32, (plan.groups, plan.wide), 1) % plan.width // plan.block
    for z in range(zl):
        parts = []
        for part in (high, low):
            piece = part[z * yl : (z + 1) * yl]
            parts.append(
                jnp.concatenate([piece[:, : plan.wide], piece[:, plan.wide :]], axis=0)
            )
        stack = jnp.concatenate([parts[0], parts[1], parts[0]], axis=0).astype(jnp.bfloat16)
        planes = mm(second[...], stack)
        for k in range(2):
            total = None
            for i in range(plan.rows_ky):
                start = (k * plan.rows_ky + i) * plan.groups
                piece = planes[start : start + plan.groups]
                total = piece if total is None else jnp.where(upper == i, piece, total)
            for s in range(plan.slabs):
                send[s, :, 2 * z + k, :] = total[:, s * 128 : (s + 1) * 128]

    pl.semaphore_wait(barrier, plan.count - 1)
    used = pl.ds(0, plan.rows)
    for offset in offsets:
        to = spread(offset)
        pltpu.make_async_remote_copy(
            src_ref=send.at[to[2], to[0] * plan.pens + to[1], used],
            dst_ref=recv.at[me, used],
            send_sem=send_sem,
            recv_sem=recv_sem,
            device_id=to,
            device_id_type=pl.DeviceIdType.MESH,
        ).start()
    recv[me, 0 : plan.rows] = send[slab, group, 0 : plan.rows]

    bm, ky_n, width = plan.block, plan.rows_ky, plan.width

    def signed(index):
        return jnp.where(index < keep // 2, index, index - keep)

    row = lax.broadcasted_iota(jnp.int32, (width, keep), 0)
    kx = signed(row % bm + slab * bm)
    ky = signed(row // bm + group * ky_n)
    kz = signed(lax.broadcasted_iota(jnp.int32, (width, keep), 1))
    limit = -(keep // 2)
    mask = ((kx != limit) & (ky != limit) & (kz != limit)).astype(jnp.float32)
    waves = [k.astype(jnp.float32) for k in (kx, ky, kz)]
    ksq = waves[0] * waves[0] + waves[1] * waves[1] + waves[2] * waves[2]
    inverse = 1.0 / jnp.maximum(ksq, 1.0)
    damp = (0.5 / (keep // 2) ** 2) * ksq
    for load in late_loads:
        load.wait()
    damped = [
        [
            jnp.concatenate([modes[c, i, k] for i in range(ky_n)], axis=0) * damp
            for k in range(2)
        ]
        for c in range(3)
    ]

    arrived = recv.at[pl.ds(0, plan.count - 1), used]
    pltpu.make_async_copy(arrived, arrived, recv_sem).wait()
    got = split_in_kernel(recv[...].reshape(plan.count * 8, 128))
    out = split_dot((third[0], third[1]), got)
    for k in range(2):
        turned = jnp.transpose(out[k * keep : (k + 1) * keep])
        comp = [turned[c * width : (c + 1) * width] for c in range(3)]
        inner = (waves[0] * comp[0] + waves[1] * comp[1] + waves[2] * comp[2]) * inverse
        for c in range(3):
            result = (comp[c] - waves[c] * inner) * mask - damped[c][k]
            for i in range(ky_n):
                out_ref[c, i, k] = result[i * bm : (i + 1) * bm]
    pltpu.make_async_copy(arrived, arrived, send_sem).wait()


def direct(plan, tables, velocity, vorticity, velocity_modes):
    modes = jnp.transpose(velocity_modes, (0, 2, 3, 4, 1))
    first, second, third = tables
    hbm = pl.BlockSpec(memory_space=pltpu.HBM)
    out = pl.pallas_call(
        functools.partial(kernel, plan),
        out_shape=pltpu.VMEM(modes.shape, jnp.float32),
        in_specs=[hbm] * 6,
        out_specs=pl.BlockSpec(memory_space=pltpu.VMEM),
        scratch_shapes=[
            pltpu.VMEM((2,) + velocity.shape, jnp.float32),
            pltpu.VMEM(modes.shape, jnp.float32),
            pltpu.VMEM((3, 128, 2 * plan.wide), jnp.bfloat16),
            pltpu.VMEM(second.shape[1:], jnp.bfloat16),
            pltpu.VMEM(third.shape, jnp.bfloat16),
            pltpu.VMEM((3 * plan.z_rows * plan.y_rows, 128), jnp.float32),
            pltpu.VMEM((plan.slabs, plan.groups, 8, 128), jnp.float32),
            pltpu.VMEM((plan.count, 8, 128), jnp.float32),
            pltpu.SemaphoreType.DMA,
            pltpu.SemaphoreType.DMA((4,)),
            pltpu.SemaphoreType.DMA((2,)),
            pltpu.SemaphoreType.DMA,
            pltpu.SemaphoreType.DMA,
        ],
        compiler_params=pltpu.CompilerParams(collective_id=0, has_side_effects=True),
    )(velocity, vorticity, modes, first, second, third)
    return jnp.transpose(out, (0, 4, 1, 2, 3))


def solution(mesh):
    sizes = dict(mesh.shape)

    def run(velocity, vorticity, velocity_modes):
        _, z_rows, y_rows, cells = velocity.shape
        plan = Plan(sizes, cells, velocity_modes.shape[1], z_rows, y_rows)
        if not plan.fits():
            return per_device(velocity, vorticity, velocity_modes)
        return direct(plan, plan.tables(), velocity, vorticity, velocity_modes)

    return jax.shard_map(
        run,
        mesh=mesh,
        in_specs=(
            P(None, ("section", "pen"), "slab", None),
            P(None, ("section", "pen"), "slab", None),
            P(None, None, ("section", "pen"), None, "slab"),
        ),
        out_specs=P(None, None, ("section", "pen"), None, "slab"),
        check_vma=False,
    )
```

time: 13.4 us -> 11.9 us (0.89)
  Pallas kernels: 12.6 us -> 11.1 us
    pallas_call x1, Pallas kernels: 12.6 us -> 11.1 us  [direct(): pl.pallas_call(functools.partial(kernel, plan), out_shape=pltpu.VMEM(mode...]
where the time goes in v1:
time: 11.9 us; the launch traced here: 11.7 us
  Pallas kernels  11.1 us (93%)
  local copies, waits for them, and re-layouts  0.64 us (5%)
    pallas_call x1, Pallas kernels, direct(): pl.pallas_call(functools.partial(kernel, plan), out_shape=pltpu.VMEM(mode...  11.1 us
    unnamed x1, local copies, waits for them, and re-layouts  0.64 us

profile of v1, /device:TPU:0, one launch (start us, length us, event | category | flops | bytes accessed | tf_op | source)
XLA Modules:
  0.0 11.7 jit_solution(34770248370086147)
XLA Ops:
  0.0 11.1 %shard_map.64 = f32[3,2,2,16,32]{4,3,2,1,0:T(8,128)S(1)} custom-call(f32[3,3,24,48]{3,2,1,0:T(8,128)} %vel_hbm.1, f32[3,3,24,48]{3,2,1,0:T(8,128)} %vort_hbm.1, f32[3,2,2,16,32]{4,3,2,1,0:T(8,128)} %bitcast.3, bf16[2,48,512]{2,1,0:T(8,128)(2,1)} %constant.6.clone.first_hbm, bf16[2,64,144]{2,1,0:T(8,128)(2,1)} %constant.7.clone.second_hbm, ...), custom_call_target="tpu_custom_call" | custom-call | tf_op jit(solution)/shard_map/pallas_call | solution.py:344
  11.1 0.6 %copy.8 = f32[3,32,2,2,16]{1,4,3,2,0:T(8,128)} copy(f32[3,32,2,2,16]{1,4,3,2,0:T(8,128)S(1)} %bitcast.2) | data formatting | bytes 49152

commit v2 on v1

--- a/solution.py
+++ b/solution.py
@@ -133,8 +133,18 @@
     return np.cos(angles) * factor, np.sin(angles) * factor
 
 
+def by_distance(devices):
+    origin = getattr(devices.flat[0], "coords", ())
+
+    def hops(index):
+        return sum(abs(a - b) for a, b in zip(getattr(devices[index], "coords", ()), origin))
+
+    return sorted(np.ndindex(devices.shape), key=lambda index: (hops(index), index))
+
+
 class Plan:
-    def __init__(self, mesh_shape, cells, keep, z_rows, y_rows):
+    def __init__(self, mesh_shape, order, cells, keep, z_rows, y_rows):
+        self.order = order
         self.cells, self.keep, self.z_rows, self.y_rows = cells, keep, z_rows, y_rows
         self.halves, self.pens, self.slabs = (mesh_shape[a] for a in AXES)
         self.groups = self.halves * self.pens
@@ -219,26 +229,19 @@
     for load in table_loads + late_loads:
         load.start()
 
-    def spread(offset):
-        a, b, c = offset
-        return (
-            lax.rem(sec + a, plan.halves),
-            lax.rem(pen + b, plan.pens),
-            lax.rem(slab + c, plan.slabs),
-        )
-
-    offsets = [
-        (a, b, c)
-        for b in sorted(range(plan.pens), key=lambda v: -min(v, plan.pens - v))
-        for a in reversed(range(plan.halves))
-        for c in reversed(range(plan.slabs))
-    ]
-    offsets.remove((0, 0, 0))
     barrier = pltpu.get_barrier_semaphore()
-    for offset in offsets:
-        pl.semaphore_signal(
-            barrier, inc=1, device_id=spread(offset), device_id_type=pl.DeviceIdType.MESH
-        )
+
+    def place(to):
+        return (to[0] * plan.pens + to[1]) * plan.slabs + to[2]
+
+    for to in reversed(plan.order):
+
+        @pl.when(me != place(to))
+        def _(to=to):
+            pl.semaphore_signal(
+                barrier, inc=1, device_id=to, device_id_type=pl.DeviceIdType.MESH
+            )
+
     if plan.rows < 8:
         recv[:, plan.rows : 8] = jnp.zeros((plan.count, 8 - plan.rows, 128), jnp.float32)
     cross[...] = jnp.zeros_like(cross)
@@ -281,21 +284,30 @@
                 piece = planes[start : start + plan.groups]
                 total = piece if total is None else jnp.where(upper == i, piece, total)
             for s in range(plan.slabs):
-                send[s, :, 2 * z + k, :] = total[:, s * 128 : (s + 1) * 128]
+                rows = pl.ds(s * plan.groups * 8 + 2 * z + k, plan.groups, stride=8)
+                send[rows, :] = total[:, s * 128 : (s + 1) * 128]
 
     pl.semaphore_wait(barrier, plan.count - 1)
     used = pl.ds(0, plan.rows)
-    for offset in offsets:
-        to = spread(offset)
-        pltpu.make_async_remote_copy(
-            src_ref=send.at[to[2], to[0] * plan.pens + to[1], used],
-            dst_ref=recv.at[me, used],
-            send_sem=send_sem,
-            recv_sem=recv_sem,
-            device_id=to,
-            device_id_type=pl.DeviceIdType.MESH,
-        ).start()
-    recv[me, 0 : plan.rows] = send[slab, group, 0 : plan.rows]
+
+    def slot_of(s, g):
+        return (s * plan.groups + g) * 8
+
+    for to in plan.order:
+
+        @pl.when(me != place(to))
+        def _(to=to):
+            pltpu.make_async_remote_copy(
+                src_ref=send.at[pl.ds(slot_of(to[2], to[0] * plan.pens + to[1]), plan.rows)],
+                dst_ref=recv.at[me, used],
+                send_sem=send_sem,
+                recv_sem=recv_sem,
+                device_id=to,
+                device_id_type=pl.DeviceIdType.MESH,
+            ).start()
+
+    own = pl.multiple_of(slot_of(slab, group), 8)
+    recv[me, 0 : plan.rows] = send[pl.ds(own, plan.rows)]
 
     bm, ky_n, width = plan.block, plan.rows_ky, plan.width
 
@@ -353,7 +365,7 @@
             pltpu.VMEM(second.shape[1:], jnp.bfloat16),
             pltpu.VMEM(third.shape, jnp.bfloat16),
             pltpu.VMEM((3 * plan.z_rows * plan.y_rows, 128), jnp.float32),
-            pltpu.VMEM((plan.slabs, plan.groups, 8, 128), jnp.float32),
+            pltpu.VMEM((plan.slabs * plan.groups * 8, 128), jnp.float32),
             pltpu.VMEM((plan.count, 8, 128), jnp.float32),
             pltpu.SemaphoreType.DMA,
             pltpu.SemaphoreType.DMA((4,)),
@@ -368,10 +380,11 @@
 
 def solution(mesh):
     sizes = dict(mesh.shape)
+    order = by_distance(mesh.devices)
 
     def run(velocity, vorticity, velocity_modes):
         _, z_rows, y_rows, cells = velocity.shape
-        plan = Plan(sizes, cells, velocity_modes.shape[1], z_rows, y_rows)
+        plan = Plan(sizes, order, cells, velocity_modes.shape[1], z_rows, y_rows)
         if not plan.fits():
             return per_device(velocity, vorticity, velocity_modes)
         return direct(plan, plan.tables(), velocity, vorticity, velocity_modes)

time: 11.9 us -> 11.1 us (0.933)
  Pallas kernels: 11.1 us -> 10.3 us
    pallas_call x1, Pallas kernels: 11.1 us -> 10.3 us  [direct(): pl.pallas_call(functools.partial(kernel, plan), out_shape=pltpu.VMEM(mode...]
where the time goes in v2:
time: 11.1 us; the launch traced here: 11 us
  Pallas kernels  10.3 us (93%)
  local copies, waits for them, and re-layouts  0.64 us (6%)
    pallas_call x1, Pallas kernels, direct(): pl.pallas_call(functools.partial(kernel, plan), out_shape=pltpu.VMEM(mode...  10.3 us
    unnamed x1, local copies, waits for them, and re-layouts  0.64 us

profile of v2, /device:TPU:0, one launch (start us, length us, event | category | flops | bytes accessed | tf_op | source)
XLA Modules:
  0.0 11.0 jit_solution(11605374530646392355)
XLA Ops:
  0.0 10.3 %shard_map.64 = f32[3,2,2,16,32]{4,3,2,1,0:T(8,128)S(1)} custom-call(f32[3,3,24,48]{3,2,1,0:T(8,128)} %vel_hbm.1, f32[3,3,24,48]{3,2,1,0:T(8,128)} %vort_hbm.1, f32[3,2,2,16,32]{4,3,2,1,0:T(8,128)} %bitcast.3, bf16[2,48,512]{2,1,0:T(8,128)(2,1)} %constant.6.clone.first_hbm, bf16[2,64,144]{2,1,0:T(8,128)(2,1)} %constant.7.clone.second_hbm, ...), custom_call_target="tpu_custom_call" | custom-call | tf_op jit(solution)/shard_map/pallas_call | solution.py:356
  10.4 0.6 %copy.8 = f32[3,32,2,2,16]{1,4,3,2,0:T(8,128)} copy(f32[3,32,2,2,16]{1,4,3,2,0:T(8,128)S(1)} %bitcast.2) | data formatting | bytes 49152

commit v3 on v2

--- a/solution.py
+++ b/solution.py
@@ -197,16 +197,23 @@
             third[1, :, :, :, 2 * z], third[1, :, :, :, 2 * z + 1] = -n, c
         third = third.reshape(2 * self.keep, self.count * 8)
         high, low = split_bf16(second)
+        kept = (self.order[0][0] * self.pens + self.order[0][1]) * ky_n
+        near = np.zeros((self.slabs, ky_n, 2, yl, 128), np.float32)
+        for s in range(self.slabs):
+            for k in range(ky_n):
+                near[s, k, 0] = cos[kept + k, s * yl : (s + 1) * yl, None]
+                near[s, k, 1] = sin[kept + k, s * yl : (s + 1) * yl, None]
         return (
             np.stack(split_bf16(first)),
             np.concatenate([high, high, low], axis=2),
             np.stack(split_bf16(third)),
+            near,
         )
 
 
 def kernel(
-    plan, vel_hbm, vort_hbm, modes_hbm, first_hbm, second_hbm, third_hbm, out_ref,
-    fields, modes, first, second, third, cross, send, recv,
+    plan, vel_hbm, vort_hbm, modes_hbm, first_hbm, second_hbm, third_hbm, near_hbm, out_ref,
+    fields, modes, first, second, third, near, cross, quick, send, recv,
     field_sem, table_sem, late_sem, send_sem, recv_sem,
 ):
     sec, pen, slab = (lax.axis_index(a) for a in AXES)
@@ -218,15 +225,15 @@
             pltpu.make_async_copy(source.at[c], fields.at[i, c], field_sem).start()
     table_loads = [
         pltpu.make_async_copy(first_hbm.at[0], first.at[0, 0:cells], table_sem.at[0]),
-        pltpu.make_async_copy(first_hbm.at[0], first.at[1, 0:cells], table_sem.at[1]),
-        pltpu.make_async_copy(first_hbm.at[1], first.at[2, 0:cells], table_sem.at[2]),
-        pltpu.make_async_copy(second_hbm.at[slab], second, table_sem.at[3]),
+        pltpu.make_async_copy(first_hbm.at[1], first.at[1, 0:cells], table_sem.at[1]),
+        pltpu.make_async_copy(second_hbm.at[slab], second, table_sem.at[2]),
+        pltpu.make_async_copy(near_hbm.at[slab], near, table_sem.at[3]),
     ]
     late_loads = [
         pltpu.make_async_copy(third_hbm, third, late_sem.at[0]),
         pltpu.make_async_copy(modes_hbm, modes, late_sem.at[1]),
     ]
-    for load in table_loads + late_loads:
+    for load in table_loads:
         load.start()
 
     barrier = pltpu.get_barrier_semaphore()
@@ -246,10 +253,12 @@
         recv[:, plan.rows : 8] = jnp.zeros((plan.count, 8 - plan.rows, 128), jnp.float32)
     cross[...] = jnp.zeros_like(cross)
     if cells < 128:
-        for i in range(3):
+        for i in range(2):
             first[i, cells:128] = jnp.zeros((128 - cells, first.shape[2]), jnp.bfloat16)
 
     pltpu.make_async_copy(fields, fields, field_sem).wait()
+    for load in late_loads:
+        load.start()
     zl, yl = plan.z_rows, plan.y_rows
     area = zl * yl
     v, w = ([fields[i, c].reshape(area, cells) for c in range(3)] for i in range(2))
@@ -258,10 +267,69 @@
         cross[c * area : (c + 1) * area, 0:cells] = v[p] * w[q] - v[q] * w[p]
     for load in table_loads:
         load.wait()
+    sub = lax.broadcasted_iota(jnp.int32, (8, 128), 0)
+    blocks = []
+    for i in range(plan.rows_ky):
+        for c in range(3):
+            block = None
+            for z in range(zl):
+                start = (c * zl + z) * yl
+                pair = []
+                for k in range(2):
+                    terms = cross[start : start + yl] * near[i, k]
+                    part = terms[0:8]
+                    for r in range(8, yl, 8):
+                        part = part + terms[r : r + 8]
+                    pair.append(part)
+                part = jnp.where(sub < 4, pair[0], pair[1]) + pltpu.roll(
+                    jnp.where(sub < 4, pair[1], pair[0]), 4, 0
+                )
+                part = part + pltpu.roll(part, 6, 0)
+                part = part + pltpu.roll(part, 7, 0)
+                if z == 0:
+                    block = part
+                else:
+                    block = jnp.where(sub % 4 == z, pltpu.roll(part, z, 0), block)
+            blocks.append(block)
+    high, low = split_in_kernel(jnp.concatenate(blocks, axis=0))
+    doubled = jnp.concatenate([first[0], first[0]], axis=0)
+    planes = mm(jnp.concatenate([high, low], axis=1), doubled) + mm(high, first[1])
+    cell = lax.broadcasted_iota(jnp.int32, (8, 2 * plan.wide), 1) % 128 // plan.block
+    total = planes[0:8]
+    for i in range(plan.rows_ky):
+        for c in range(3):
+            start = (i * 3 + c) * 8
+            total = jnp.where(cell == c * plan.rows_ky + i, planes[start : start + 8], total)
+    real, imag = total[:, : plan.wide], total[:, plan.wide :]
+    parts = (real + pltpu.roll(imag, 4, 0), imag - pltpu.roll(real, 4, 0))
+    for k in range(2):
+        for s in range(plan.slabs):
+            quick[pl.ds(s * 8 + k, zl, stride=2), :] = parts[k][0:zl, s * 128 : (s + 1) * 128]
+
+    pl.semaphore_wait(barrier, plan.count - 1)
+    used = pl.ds(0, plan.rows)
+
+    def slot_of(s, g):
+        return (s * plan.groups + g) * 8
+
+    for s in range(plan.slabs):
+        to = (*plan.order[0][:2], s)
+
+        @pl.when(me != place(to))
+        def _(to=to):
+            pltpu.make_async_remote_copy(
+                src_ref=quick.at[pl.ds(to[2] * 8, plan.rows)],
+                dst_ref=recv.at[me, used],
+                send_sem=send_sem,
+                recv_sem=recv_sem,
+                device_id=to,
+                device_id_type=pl.DeviceIdType.MESH,
+            ).start()
+
     high, low = split_in_kernel(cross[...])
     along_x = mm(
-        jnp.concatenate([high, low], axis=1), jnp.concatenate([first[0], first[1]], axis=0)
-    ) + mm(high, first[2])
+        jnp.concatenate([high, low], axis=1), jnp.concatenate([first[0], first[0]], axis=0)
+    ) + mm(high, first[1])
     slot = lax.broadcasted_iota(jnp.int32, (area, 2 * plan.wide), 1) % 128 // plan.width
     along_x = [along_x[c * area : (c + 1) * area] for c in range(3)]
     along_x = jnp.where(slot == 0, along_x[0], jnp.where(slot == 1, along_x[1], along_x[2]))
@@ -287,13 +355,7 @@
                 rows = pl.ds(s * plan.groups * 8 + 2 * z + k, plan.groups, stride=8)
                 send[rows, :] = total[:, s * 128 : (s + 1) * 128]
 
-    pl.semaphore_wait(barrier, plan.count - 1)
-    used = pl.ds(0, plan.rows)
-
-    def slot_of(s, g):
-        return (s * plan.groups + g) * 8
-
-    for to in plan.order:
+    for to in plan.order[plan.slabs :]:
 
         @pl.when(me != place(to))
         def _(to=to):
@@ -337,7 +399,8 @@
     arrived = recv.at[pl.ds(0, plan.count - 1), used]
     pltpu.make_async_copy(arrived, arrived, recv_sem).wait()
     got = split_in_kernel(recv[...].reshape(plan.count * 8, 128))
-    out = split_dot((third[0], third[1]), got)
+    wide_ = mm(third[0], jnp.concatenate([got[0], got[1]], axis=1))
+    out = wide_[:, :128] + wide_[:, 128:] + mm(third[1], got[0])
     for k in range(2):
         turned = jnp.transpose(out[k * keep : (k + 1) * keep])
         comp = [turned[c * width : (c + 1) * width] for c in range(3)]
@@ -351,20 +414,22 @@
 
 def direct(plan, tables, velocity, vorticity, velocity_modes):
     modes = jnp.transpose(velocity_modes, (0, 2, 3, 4, 1))
-    first, second, third = tables
+    first, second, third, near = tables
     hbm = pl.BlockSpec(memory_space=pltpu.HBM)
     out = pl.pallas_call(
         functools.partial(kernel, plan),
         out_shape=pltpu.VMEM(modes.shape, jnp.float32),
-        in_specs=[hbm] * 6,
+        in_specs=[hbm] * 7,
         out_specs=pl.BlockSpec(memory_space=pltpu.VMEM),
         scratch_shapes=[
             pltpu.VMEM((2,) + velocity.shape, jnp.float32),
             pltpu.VMEM(modes.shape, jnp.float32),
-            pltpu.VMEM((3, 128, 2 * plan.wide), jnp.bfloat16),
+            pltpu.VMEM((2, 128, 2 * plan.wide), jnp.bfloat16),
             pltpu.VMEM(second.shape[1:], jnp.bfloat16),
             pltpu.VMEM(third.shape, jnp.bfloat16),
+            pltpu.VMEM(near.shape[1:], jnp.float32),
             pltpu.VMEM((3 * plan.z_rows * plan.y_rows, 128), jnp.float32),
+            pltpu.VMEM((plan.slabs * 8, 128), jnp.float32),
             pltpu.VMEM((plan.slabs * plan.groups * 8, 128), jnp.float32),
             pltpu.VMEM((plan.count, 8, 128), jnp.float32),
             pltpu.SemaphoreType.DMA,
@@ -374,7 +439,7 @@
             pltpu.SemaphoreType.DMA,
         ],
         compiler_params=pltpu.CompilerParams(collective_id=0, has_side_effects=True),
-    )(velocity, vorticity, modes, first, second, third)
+    )(velocity, vorticity, modes, first, second, third, near)
     return jnp.transpose(out, (0, 4, 1, 2, 3))
 
 

time: 11.1 us -> 10.9 us (0.982)
  Pallas kernels: 10.3 us -> 10.1 us
    pallas_call x1, Pallas kernels: 10.3 us -> 10.1 us  [direct(): pl.pallas_call(functools.partial(kernel, plan), out_shape=pltpu.VMEM(mode...]
where the time goes in v3:
time: 10.9 us; the launch traced here: 10.8 us
  Pallas kernels  10.1 us (93%)
  local copies, waits for them, and re-layouts  0.64 us (6%)
    pallas_call x1, Pallas kernels, direct(): pl.pallas_call(functools.partial(kernel, plan), out_shape=pltpu.VMEM(mode...  10.1 us
    unnamed x1, local copies, waits for them, and re-layouts  0.64 us

profile of v3, /device:TPU:0, one launch (start us, length us, event | category | flops | bytes accessed | tf_op | source)
XLA Modules:
  0.0 10.8 jit_solution(1326197581305574425)
XLA Ops:
  0.0 10.1 %shard_map.73 = f32[3,2,2,16,32]{4,3,2,1,0:T(8,128)S(1)} custom-call(f32[3,3,24,48]{3,2,1,0:T(8,128)} %vel_hbm.1, f32[3,3,24,48]{3,2,1,0:T(8,128)} %vort_hbm.1, f32[3,2,2,16,32]{4,3,2,1,0:T(8,128)} %bitcast.3, bf16[2,48,512]{2,1,0:T(8,128)(2,1)} %constant.8.clone.first_hbm, bf16[2,64,144]{2,1,0:T(8,128)(2,1)} %constant.9.clone.second_hbm, ...), custom_call_target="tpu_custom_call" | custom-call | tf_op jit(solution)/shard_map/pallas_call | solution.py:419
  10.1 0.6 %copy.9 = f32[3,32,2,2,16]{1,4,3,2,0:T(8,128)} copy(f32[3,32,2,2,16]{1,4,3,2,0:T(8,128)S(1)} %bitcast.2) | data formatting | bytes 49152

commit v4 on v3

--- a/solution.py
+++ b/solution.py
@@ -137,9 +137,18 @@
     origin = getattr(devices.flat[0], "coords", ())
 
     def hops(index):
-        return sum(abs(a - b) for a, b in zip(getattr(devices[index], "coords", ()), origin))
-
-    return sorted(np.ndindex(devices.shape), key=lambda index: (hops(index), index))
+        return [abs(a - b) for a, b in zip(getattr(devices[index], "coords", ()), origin)]
+
+    every = list(np.ndindex(devices.shape))
+    spans = [max(far) for far in zip(*map(hops, every))]
+
+    def key(index):
+        far = hops(index)
+        if sum(far) == 0:
+            return -1, 0, index
+        return (far[spans.index(max(spans))], -sum(far), index) if far else (0, 0, index)
+
+    return sorted(every, key=key)
 
 
 class Plan:
@@ -195,6 +204,17 @@
             c, n = cos[:, z::zl][:, :, None], sin[:, z::zl][:, :, None]
             third[0, :, :, :, 2 * z], third[0, :, :, :, 2 * z + 1] = c, n
             third[1, :, :, :, 2 * z], third[1, :, :, :, 2 * z + 1] = -n, c
+        final = third[:, :, g - 1, 0, : self.rows].reshape(2 * self.keep, self.rows)
+        final = np.ascontiguousarray(np.broadcast_to(final.T[:, :, None], (*final.T.shape, 128)))
+        third = third.reshape(2 * self.keep, self.count * 8)
+        high, low = split_bf16(second)
+        third = np.zeros((2, self.keep, g, self.slabs, 8), np.float32)
+        for z in range(zl):
+            c, n = cos[:, z::zl][:, :, None], sin[:, z::zl][:, :, None]
+            third[0, :, :, :, 2 * z], third[0, :, :, :, 2 * z + 1] = c, n
+            third[1, :, :, :, 2 * z], third[1, :, :, :, 2 * z + 1] = -n, c
+        final = third[:, :, g - 1, 0, : self.rows].reshape(2 * self.keep, self.rows)
+        final = np.ascontiguousarray(np.broadcast_to(final.T[:, :, None], (*final.T.shape, 128)))
         third = third.reshape(2 * self.keep, self.count * 8)
         high, low = split_bf16(second)
         kept = (self.order[0][0] * self.pens + self.order[0][1]) * ky_n
@@ -206,19 +226,21 @@
         return (
             np.stack(split_bf16(first)),
             np.concatenate([high, high, low], axis=2),
-            np.stack(split_bf16(third)),
-            near,
+            np.stack(split_bf16(third[:, : (g - 1) * self.slabs * 8])),
+            final,
         )
 
 
 def kernel(
-    plan, vel_hbm, vort_hbm, modes_hbm, first_hbm, second_hbm, third_hbm, near_hbm, out_ref,
-    fields, modes, first, second, third, near, cross, quick, send, recv,
+    plan, vel_hbm, vort_hbm, modes_hbm, first_hbm, second_hbm, third_hbm, final_hbm, out_ref,
+    fields, modes, first, second, third, near, final, cross, quick, send, recv,
     field_sem, table_sem, late_sem, send_sem, recv_sem,
 ):
     sec, pen, slab = (lax.axis_index(a) for a in AXES)
     group = sec * plan.pens + pen
     me = group * plan.slabs + slab
+    kind = group // (plan.groups - 1)
+    is_last = kind == 1
     cells, keep = plan.cells, plan.keep
     for i, source in enumerate((vel_hbm, vort_hbm)):
         for c in range(3):
@@ -226,12 +248,12 @@
     table_loads = [
         pltpu.make_async_copy(first_hbm.at[0], first.at[0, 0:cells], table_sem.at[0]),
         pltpu.make_async_copy(first_hbm.at[1], first.at[1, 0:cells], table_sem.at[1]),
-        pltpu.make_async_copy(second_hbm.at[slab], second, table_sem.at[2]),
-        pltpu.make_async_copy(near_hbm.at[slab], near, table_sem.at[3]),
     ]
     late_loads = [
-        pltpu.make_async_copy(third_hbm, third, late_sem.at[0]),
-        pltpu.make_async_copy(modes_hbm, modes, late_sem.at[1]),
+        pltpu.make_async_copy(second_hbm.at[slab], second, late_sem.at[0]),
+        pltpu.make_async_copy(third_hbm, third, late_sem.at[1]),
+        pltpu.make_async_copy(modes_hbm, modes, late_sem.at[2]),
+        pltpu.make_async_copy(final_hbm, final, late_sem.at[3]),
     ]
     for load in table_loads:
         load.start()
@@ -252,6 +274,13 @@
     if plan.rows < 8:
         recv[:, plan.rows : 8] = jnp.zeros((plan.count, 8 - plan.rows, 128), jnp.float32)
     cross[...] = jnp.zeros_like(cross)
+    kept = plan.order[0][0] * plan.pens + plan.order[0][1]
+    line = lax.broadcasted_iota(jnp.int32, (plan.y_rows, 128), 0) + slab * plan.y_rows
+    for i in range(plan.rows_ky):
+        wave = int(wave_numbers(keep)[kept * plan.rows_ky + i])
+        angle = (wave * line % cells).astype(jnp.float32) * (2.0 * math.pi / cells)
+        near[i, 0] = jnp.cos(angle) * (1.0 / math.sqrt(cells))
+        near[i, 1] = jnp.sin(angle) * (1.0 / math.sqrt(cells))
     if cells < 128:
         for i in range(2):
             first[i, cells:128] = jnp.zeros((128 - cells, first.shape[2]), jnp.bfloat16)
@@ -292,8 +321,10 @@
                     block = jnp.where(sub % 4 == z, pltpu.roll(part, z, 0), block)
             blocks.append(block)
     high, low = split_in_kernel(jnp.concatenate(blocks, axis=0))
-    doubled = jnp.concatenate([first[0], first[0]], axis=0)
-    planes = mm(jnp.concatenate([high, low], axis=1), doubled) + mm(high, first[1])
+    planes = mm(
+        jnp.concatenate([high, low, high], axis=1),
+        jnp.concatenate([first[0], first[0], first[1]], axis=0),
+    )
     cell = lax.broadcasted_iota(jnp.int32, (8, 2 * plan.wide), 1) % 128 // plan.block
     total = planes[0:8]
     for i in range(plan.rows_ky):
@@ -321,7 +352,7 @@
                 src_ref=quick.at[pl.ds(to[2] * 8, plan.rows)],
                 dst_ref=recv.at[me, used],
                 send_sem=send_sem,
-                recv_sem=recv_sem,
+                recv_sem=recv_sem.at[kind],
                 device_id=to,
                 device_id_type=pl.DeviceIdType.MESH,
             ).start()
@@ -330,6 +361,7 @@
     along_x = mm(
         jnp.concatenate([high, low], axis=1), jnp.concatenate([first[0], first[0]], axis=0)
     ) + mm(high, first[1])
+    late_loads[0].wait()
     slot = lax.broadcasted_iota(jnp.int32, (area, 2 * plan.wide), 1) % 128 // plan.width
     along_x = [along_x[c * area : (c + 1) * area] for c in range(3)]
     along_x = jnp.where(slot == 0, along_x[0], jnp.where(slot == 1, along_x[1], along_x[2]))
@@ -363,7 +395,7 @@
                 src_ref=send.at[pl.ds(slot_of(to[2], to[0] * plan.pens + to[1]), plan.rows)],
                 dst_ref=recv.at[me, used],
                 send_sem=send_sem,
-                recv_sem=recv_sem,
+                recv_sem=recv_sem.at[kind],
                 device_id=to,
                 device_id_type=pl.DeviceIdType.MESH,
             ).start()
@@ -386,7 +418,7 @@
     ksq = waves[0] * waves[0] + waves[1] * waves[1] + waves[2] * waves[2]
     inverse = 1.0 / jnp.maximum(ksq, 1.0)
     damp = (0.5 / (keep // 2) ** 2) * ksq
-    for load in late_loads:
+    for load in late_loads[1:]:
         load.wait()
     damped = [
         [
@@ -396,11 +428,38 @@
         for c in range(3)
     ]
 
-    arrived = recv.at[pl.ds(0, plan.count - 1), used]
-    pltpu.make_async_copy(arrived, arrived, recv_sem).wait()
-    got = split_in_kernel(recv[...].reshape(plan.count * 8, 128))
-    wide_ = mm(third[0], jnp.concatenate([got[0], got[1]], axis=1))
-    out = wide_[:, :128] + wide_[:, 128:] + mm(third[1], got[0])
+    def landed(messages, sem):
+        part = recv.at[pl.ds(0, messages), used]
+        pltpu.make_async_copy(part, part, sem).wait()
+
+    early = plan.count - plan.slabs
+
+    @pl.when(is_last)
+    def _():
+        landed(early, recv_sem.at[0])
+
+    @pl.when(jnp.logical_not(is_last))
+    def _():
+        landed(early - 1, recv_sem.at[0])
+
+    got = split_in_kernel(recv[0:early].reshape(early * 8, 128))
+    out = mm(third[0], jnp.concatenate(got, axis=1))
+    out = out[:, :128] + out[:, 128:] + mm(third[1], got[0])
+
+    @pl.when(is_last)
+    def _():
+        if plan.slabs > 1:
+            landed(plan.slabs - 1, recv_sem.at[1])
+
+    @pl.when(jnp.logical_not(is_last))
+    def _():
+        landed(plan.slabs, recv_sem.at[1])
+
+    tail = recv[early]
+    for s in range(1, plan.slabs):
+        tail = tail + recv[early + s]
+    for r in range(plan.rows):
+        out = out + final[r] * tail[r : r + 1]
     for k in range(2):
         turned = jnp.transpose(out[k * keep : (k + 1) * keep])
         comp = [turned[c * width : (c + 1) * width] for c in range(3)]
@@ -409,12 +468,12 @@
             result = (comp[c] - waves[c] * inner) * mask - damped[c][k]
             for i in range(ky_n):
                 out_ref[c, i, k] = result[i * bm : (i + 1) * bm]
-    pltpu.make_async_copy(arrived, arrived, send_sem).wait()
+    landed(plan.count - 1, send_sem)
 
 
 def direct(plan, tables, velocity, vorticity, velocity_modes):
     modes = jnp.transpose(velocity_modes, (0, 2, 3, 4, 1))
-    first, second, third, near = tables
+    first, second, third, final = tables
     hbm = pl.BlockSpec(memory_space=pltpu.HBM)
     out = pl.pallas_call(
         functools.partial(kernel, plan),
@@ -427,19 +486,20 @@
             pltpu.VMEM((2, 128, 2 * plan.wide), jnp.bfloat16),
             pltpu.VMEM(second.shape[1:], jnp.bfloat16),
             pltpu.VMEM(third.shape, jnp.bfloat16),
-            pltpu.VMEM(near.shape[1:], jnp.float32),
+            pltpu.VMEM((plan.rows_ky, 2, plan.y_rows, 128), jnp.float32),
+            pltpu.VMEM(final.shape, jnp.float32),
             pltpu.VMEM((3 * plan.z_rows * plan.y_rows, 128), jnp.float32),
             pltpu.VMEM((plan.slabs * 8, 128), jnp.float32),
             pltpu.VMEM((plan.slabs * plan.groups * 8, 128), jnp.float32),
             pltpu.VMEM((plan.count, 8, 128), jnp.float32),
             pltpu.SemaphoreType.DMA,
+            pltpu.SemaphoreType.DMA((2,)),
             pltpu.SemaphoreType.DMA((4,)),
+            pltpu.SemaphoreType.DMA,
             pltpu.SemaphoreType.DMA((2,)),
-            pltpu.SemaphoreType.DMA,
-            pltpu.SemaphoreType.DMA,
         ],
         compiler_params=pltpu.CompilerParams(collective_id=0, has_side_effects=True),
-    )(velocity, vorticity, modes, first, second, third, near)
+    )(velocity, vorticity, modes, first, second, third, final)
     return jnp.transpose(out, (0, 4, 1, 2, 3))
 
 

time: 10.9 us -> 10.8 us (level)
  Pallas kernels: 10.1 us -> 9.98 us
    pallas_call x1, Pallas kernels: 10.1 us -> 9.98 us  [direct(): pl.pallas_call(functools.partial(kernel, plan), out_shape=pltpu.VMEM(mode...]
where the time goes in v4:
time: 10.8 us; the launch traced here: 10.6 us
  Pallas kernels  9.98 us (92%)
  local copies, waits for them, and re-layouts  0.64 us (6%)
    pallas_call x1, Pallas kernels, direct(): pl.pallas_call(functools.partial(kernel, plan), out_shape=pltpu.VMEM(mode...  9.98 us
    unnamed x1, local copies, waits for them, and re-layouts  0.64 us

profile of v4, /device:TPU:0, one launch (start us, length us, event | category | flops | bytes accessed | tf_op | source)
XLA Modules:
  0.0 10.6 jit_solution(3350596579097787933)
XLA Ops:
  0.0 10.0 %shard_map.73 = f32[3,2,2,16,32]{4,3,2,1,0:T(8,128)S(1)} custom-call(f32[3,3,24,48]{3,2,1,0:T(8,128)} %vel_hbm.1, f32[3,3,24,48]{3,2,1,0:T(8,128)} %vort_hbm.1, f32[3,2,2,16,32]{4,3,2,1,0:T(8,128)} %bitcast.3, bf16[2,48,512]{2,1,0:T(8,128)(2,1)} %constant.8.clone.first_hbm, bf16[2,64,144]{2,1,0:T(8,128)(2,1)} %constant.9.clone.second_hbm, ...), custom_call_target="tpu_custom_call" | custom-call | tf_op jit(solution)/shard_map/pallas_call | solution.py:478
  10.0 0.6 %copy.9 = f32[3,32,2,2,16]{1,4,3,2,0:T(8,128)} copy(f32[3,32,2,2,16]{1,4,3,2,0:T(8,128)S(1)} %bitcast.2) | data formatting | bytes 49152

commit v5 on v4

--- a/solution.py
+++ b/solution.py
@@ -184,13 +184,7 @@
 
     def tables(self):
         cos, sin = host_tables(self.cells, self.keep)
-        g, zl, yl, ky_n, bm = self.groups, self.z_rows, self.y_rows, self.rows_ky, self.block
-        first = np.zeros((self.cells, 2, self.slabs, 128 // self.width, ky_n, bm), np.float32)
-        for s in range(self.slabs):
-            modes = slice(s * bm, (s + 1) * bm)
-            first[:, 0, s, :3] = cos[modes].T[:, None, None]
-            first[:, 1, s, :3] = -sin[modes].T[:, None, None]
-        first = first.reshape(self.cells, 2 * self.wide)
+        g, zl, yl, ky_n = self.groups, self.z_rows, self.y_rows, self.rows_ky
         second = np.zeros((self.slabs, 2, ky_n, g, 2, yl), np.float32)
         for s in range(self.slabs):
             for k in range(ky_n):
@@ -224,7 +218,6 @@
                 near[s, k, 0] = cos[kept + k, s * yl : (s + 1) * yl, None]
                 near[s, k, 1] = sin[kept + k, s * yl : (s + 1) * yl, None]
         return (
-            np.stack(split_bf16(first)),
             np.concatenate([high, high, low], axis=2),
             np.stack(split_bf16(third[:, : (g - 1) * self.slabs * 8])),
             final,
@@ -232,9 +225,9 @@
 
 
 def kernel(
-    plan, vel_hbm, vort_hbm, modes_hbm, first_hbm, second_hbm, third_hbm, final_hbm, out_ref,
+    plan, vel_hbm, vort_hbm, modes_hbm, second_hbm, third_hbm, final_hbm, out_ref,
     fields, modes, first, second, third, near, final, cross, quick, send, recv,
-    field_sem, table_sem, late_sem, send_sem, recv_sem,
+    field_sem, late_sem, send_sem, recv_sem,
 ):
     sec, pen, slab = (lax.axis_index(a) for a in AXES)
     group = sec * plan.pens + pen
@@ -245,25 +238,22 @@
     for i, source in enumerate((vel_hbm, vort_hbm)):
         for c in range(3):
             pltpu.make_async_copy(source.at[c], fields.at[i, c], field_sem).start()
-    table_loads = [
-        pltpu.make_async_copy(first_hbm.at[0], first.at[0, 0:cells], table_sem.at[0]),
-        pltpu.make_async_copy(first_hbm.at[1], first.at[1, 0:cells], table_sem.at[1]),
-    ]
     late_loads = [
         pltpu.make_async_copy(second_hbm.at[slab], second, late_sem.at[0]),
         pltpu.make_async_copy(third_hbm, third, late_sem.at[1]),
         pltpu.make_async_copy(modes_hbm, modes, late_sem.at[2]),
         pltpu.make_async_copy(final_hbm, final, late_sem.at[3]),
     ]
-    for load in table_loads:
-        load.start()
 
     barrier = pltpu.get_barrier_semaphore()
+
+    def signed(index):
+        return jnp.where(index < keep // 2, index, index - keep)
 
     def place(to):
         return (to[0] * plan.pens + to[1]) * plan.slabs + to[2]
 
-    for to in reversed(plan.order):
+    for to in plan.order:
 
         @pl.when(me != place(to))
         def _(to=to):
@@ -274,13 +264,33 @@
     if plan.rows < 8:
         recv[:, plan.rows : 8] = jnp.zeros((plan.count, 8 - plan.rows, 128), jnp.float32)
     cross[...] = jnp.zeros_like(cross)
+    scale = 1.0 / math.sqrt(cells)
+
+    def turn(wave, cell):
+        product = wave * cell
+        product = product - cells * jnp.floor(product * (1.0 / cells) + 0.5)
+        angle = product * (2.0 * math.pi / cells)
+        return jnp.cos(angle) * scale, jnp.sin(angle) * scale
+
+    def ramp(shape, axis):
+        return lax.broadcasted_iota(jnp.int32, shape, axis)
+
     kept = plan.order[0][0] * plan.pens + plan.order[0][1]
-    line = lax.broadcasted_iota(jnp.int32, (plan.y_rows, 128), 0) + slab * plan.y_rows
+    line = (ramp((plan.y_rows, 128), 0) + slab * plan.y_rows).astype(jnp.float32)
+    waves_near = [float(wave_numbers(keep)[kept * plan.rows_ky + i]) for i in range(plan.rows_ky)]
     for i in range(plan.rows_ky):
-        wave = int(wave_numbers(keep)[kept * plan.rows_ky + i])
-        angle = (wave * line % cells).astype(jnp.float32) * (2.0 * math.pi / cells)
-        near[i, 0] = jnp.cos(angle) * (1.0 / math.sqrt(cells))
-        near[i, 1] = jnp.sin(angle) * (1.0 / math.sqrt(cells))
+        if waves_near[i] != 0:
+            near[i, 0], near[i, 1] = turn(waves_near[i], line)
+    lane = ramp((cells, 128), 1)
+    line = ramp((cells, 128), 0).astype(jnp.float32)
+    for s in range(plan.slabs):
+        wave = signed(lane % plan.block + s * plan.block).astype(jnp.float32)
+        cosine, sine = turn(wave, line)
+        for k, table in enumerate((cosine, -sine)):
+            table = split_in_kernel(jnp.where(lane < 3 * plan.width, table, 0.0))
+            start = k * plan.wide + s * 128
+            for i in range(2):
+                first[i, 0:cells, start : start + 128] = table[i]
     if cells < 128:
         for i in range(2):
             first[i, cells:128] = jnp.zeros((128 - cells, first.shape[2]), jnp.bfloat16)
@@ -294,31 +304,40 @@
     for c in range(3):
         p, q = (c + 1) % 3, (c + 2) % 3
         cross[c * area : (c + 1) * area, 0:cells] = v[p] * w[q] - v[q] * w[p]
-    for load in table_loads:
-        load.wait()
     sub = lax.broadcasted_iota(jnp.int32, (8, 128), 0)
+
+    def folded(terms):
+        part = terms[0:8]
+        for r in range(8, yl, 8):
+            part = part + terms[r : r + 8]
+        return part
+
     blocks = []
     for i in range(plan.rows_ky):
         for c in range(3):
-            block = None
+            sums = []
             for z in range(zl):
                 start = (c * zl + z) * yl
-                pair = []
-                for k in range(2):
-                    terms = cross[start : start + yl] * near[i, k]
-                    part = terms[0:8]
-                    for r in range(8, yl, 8):
-                        part = part + terms[r : r + 8]
-                    pair.append(part)
-                part = jnp.where(sub < 4, pair[0], pair[1]) + pltpu.roll(
-                    jnp.where(sub < 4, pair[1], pair[0]), 4, 0
-                )
-                part = part + pltpu.roll(part, 6, 0)
-                part = part + pltpu.roll(part, 7, 0)
-                if z == 0:
-                    block = part
+                line = cross[start : start + yl]
+                if waves_near[i] == 0:
+                    part = folded(line)
+                    part = part + pltpu.roll(part, 4, 0)
                 else:
-                    block = jnp.where(sub % 4 == z, pltpu.roll(part, z, 0), block)
+                    pair = [folded(line * near[i, k]) for k in range(2)]
+                    part = jnp.where(sub < 4, pair[0], pair[1]) + pltpu.roll(
+                        jnp.where(sub < 4, pair[1], pair[0]), 4, 0
+                    )
+                sums.append(part + pltpu.roll(part, 2 if z // 2 % 2 else 6, 0))
+            even, odd = None, None
+            for z in range(0, zl, 2):
+                even = sums[z] if even is None else jnp.where(sub % 4 < 2, even, sums[z])
+            for z in range(1, zl, 2):
+                odd = sums[z] if odd is None else jnp.where(sub % 4 < 2, odd, sums[z])
+            block = even + pltpu.roll(even, 7, 0)
+            if odd is not None:
+                block = jnp.where(sub % 2 == 0, block, odd + pltpu.roll(odd, 1, 0))
+            if waves_near[i] == 0:
+                block = jnp.where(sub < 4, block * scale, 0.0)
             blocks.append(block)
     high, low = split_in_kernel(jnp.concatenate(blocks, axis=0))
     planes = mm(
@@ -337,25 +356,30 @@
         for s in range(plan.slabs):
             quick[pl.ds(s * 8 + k, zl, stride=2), :] = parts[k][0:zl, s * 128 : (s + 1) * 128]
 
-    pl.semaphore_wait(barrier, plan.count - 1)
     used = pl.ds(0, plan.rows)
 
     def slot_of(s, g):
         return (s * plan.groups + g) * 8
 
-    for s in range(plan.slabs):
-        to = (*plan.order[0][:2], s)
-
-        @pl.when(me != place(to))
-        def _(to=to):
-            pltpu.make_async_remote_copy(
-                src_ref=quick.at[pl.ds(to[2] * 8, plan.rows)],
-                dst_ref=recv.at[me, used],
-                send_sem=send_sem,
-                recv_sem=recv_sem.at[kind],
-                device_id=to,
-                device_id_type=pl.DeviceIdType.MESH,
-            ).start()
+    def open_with_near():
+        pl.semaphore_wait(barrier, plan.count - 1)
+        for s in range(plan.slabs):
+            to = (*plan.order[0][:2], s)
+
+            @pl.when(me != place(to))
+            def _(to=to):
+                pltpu.make_async_remote_copy(
+                    src_ref=quick.at[pl.ds(to[2] * 8, plan.rows)],
+                    dst_ref=recv.at[me, used],
+                    send_sem=send_sem,
+                    recv_sem=recv_sem.at[kind],
+                    device_id=to,
+                    device_id_type=pl.DeviceIdType.MESH,
+                ).start()
+
+    @pl.when(is_last)
+    def _():
+        open_with_near()
 
     high, low = split_in_kernel(cross[...])
     along_x = mm(
@@ -387,6 +411,10 @@
                 rows = pl.ds(s * plan.groups * 8 + 2 * z + k, plan.groups, stride=8)
                 send[rows, :] = total[:, s * 128 : (s + 1) * 128]
 
+    @pl.when(jnp.logical_not(is_last))
+    def _():
+        open_with_near()
+
     for to in plan.order[plan.slabs :]:
 
         @pl.when(me != place(to))
@@ -404,9 +432,6 @@
     recv[me, 0 : plan.rows] = send[pl.ds(own, plan.rows)]
 
     bm, ky_n, width = plan.block, plan.rows_ky, plan.width
-
-    def signed(index):
-        return jnp.where(index < keep // 2, index, index - keep)
 
     row = lax.broadcasted_iota(jnp.int32, (width, keep), 0)
     kx = signed(row % bm + slab * bm)
@@ -473,12 +498,12 @@
 
 def direct(plan, tables, velocity, vorticity, velocity_modes):
     modes = jnp.transpose(velocity_modes, (0, 2, 3, 4, 1))
-    first, second, third, final = tables
+    second, third, final = tables
     hbm = pl.BlockSpec(memory_space=pltpu.HBM)
     out = pl.pallas_call(
         functools.partial(kernel, plan),
         out_shape=pltpu.VMEM(modes.shape, jnp.float32),
-        in_specs=[hbm] * 7,
+        in_specs=[hbm] * 6,
         out_specs=pl.BlockSpec(memory_space=pltpu.VMEM),
         scratch_shapes=[
             pltpu.VMEM((2,) + velocity.shape, jnp.float32),
@@ -493,13 +518,12 @@
             pltpu.VMEM((plan.slabs * plan.groups * 8, 128), jnp.float32),
             pltpu.VMEM((plan.count, 8, 128), jnp.float32),
             pltpu.SemaphoreType.DMA,
-            pltpu.SemaphoreType.DMA((2,)),
             pltpu.SemaphoreType.DMA((4,)),
             pltpu.SemaphoreType.DMA,
             pltpu.SemaphoreType.DMA((2,)),
         ],
         compiler_params=pltpu.CompilerParams(collective_id=0, has_side_effects=True),
-    )(velocity, vorticity, modes, first, second, third, final)
+    )(velocity, vorticity, modes, second, third, final)
     return jnp.transpose(out, (0, 4, 1, 2, 3))
 
 

time: 10.8 us -> 10.8 us (level)
  no operation moved by 1% of the time
where the time goes in v5:
time: 10.8 us; the launch traced here: 10.6 us
  Pallas kernels  9.93 us (92%)
  local copies, waits for them, and re-layouts  0.64 us (6%)
    pallas_call x1, Pallas kernels, direct(): pl.pallas_call(functools.partial(kernel, plan), out_shape=pltpu.VMEM(mode...  9.93 us
    unnamed x1, local copies, waits for them, and re-layouts  0.64 us

profile of v5, /device:TPU:0, one launch (start us, length us, event | category | flops | bytes accessed | tf_op | source)
XLA Modules:
  0.0 10.6 jit_solution(4575506097968995195)
XLA Ops:
  0.0 9.9 %shard_map.64 = f32[3,2,2,16,32]{4,3,2,1,0:T(8,128)S(1)} custom-call(f32[3,3,24,48]{3,2,1,0:T(8,128)} %vel_hbm.1, f32[3,3,24,48]{3,2,1,0:T(8,128)} %vort_hbm.1, f32[3,2,2,16,32]{4,3,2,1,0:T(8,128)} %bitcast.3, bf16[2,64,144]{2,1,0:T(8,128)(2,1)} %constant.6.clone.second_hbm, bf16[2,64,240]{2,1,0:T(8,128)(2,1)} %constant.7.clone.third_hbm, ...), custom_call_target="tpu_custom_call" | custom-call | tf_op jit(solution)/shard_map/pallas_call | solution.py:503
  9.9 0.6 %copy.8 = f32[3,32,2,2,16]{1,4,3,2,0:T(8,128)} copy(f32[3,32,2,2,16]{1,4,3,2,0:T(8,128)S(1)} %bitcast.2) | data formatting | bytes 49152

commit v6 on v5

--- a/solution.py
+++ b/solution.py
@@ -184,48 +184,20 @@
 
     def tables(self):
         cos, sin = host_tables(self.cells, self.keep)
-        g, zl, yl, ky_n = self.groups, self.z_rows, self.y_rows, self.rows_ky
-        second = np.zeros((self.slabs, 2, ky_n, g, 2, yl), np.float32)
-        for s in range(self.slabs):
-            for k in range(ky_n):
-                c = cos[k::ky_n, s * yl : (s + 1) * yl]
-                n = sin[k::ky_n, s * yl : (s + 1) * yl]
-                second[s, 0, k, :, 0], second[s, 0, k, :, 1] = c, n
-                second[s, 1, k, :, 0], second[s, 1, k, :, 1] = -n, c
-        second = second.reshape(self.slabs, 2 * self.keep, 2 * yl)
-        third = np.zeros((2, self.keep, g, self.slabs, 8), np.float32)
+        g, zl = self.groups, self.z_rows
+        table = np.zeros((2, self.keep, g, self.slabs, 8), np.float32)
         for z in range(zl):
             c, n = cos[:, z::zl][:, :, None], sin[:, z::zl][:, :, None]
-            third[0, :, :, :, 2 * z], third[0, :, :, :, 2 * z + 1] = c, n
-            third[1, :, :, :, 2 * z], third[1, :, :, :, 2 * z + 1] = -n, c
-        final = third[:, :, g - 1, 0, : self.rows].reshape(2 * self.keep, self.rows)
-        final = np.ascontiguousarray(np.broadcast_to(final.T[:, :, None], (*final.T.shape, 128)))
-        third = third.reshape(2 * self.keep, self.count * 8)
-        high, low = split_bf16(second)
-        third = np.zeros((2, self.keep, g, self.slabs, 8), np.float32)
-        for z in range(zl):
-            c, n = cos[:, z::zl][:, :, None], sin[:, z::zl][:, :, None]
-            third[0, :, :, :, 2 * z], third[0, :, :, :, 2 * z + 1] = c, n
-            third[1, :, :, :, 2 * z], third[1, :, :, :, 2 * z + 1] = -n, c
-        final = third[:, :, g - 1, 0, : self.rows].reshape(2 * self.keep, self.rows)
-        final = np.ascontiguousarray(np.broadcast_to(final.T[:, :, None], (*final.T.shape, 128)))
-        third = third.reshape(2 * self.keep, self.count * 8)
-        high, low = split_bf16(second)
-        kept = (self.order[0][0] * self.pens + self.order[0][1]) * ky_n
-        near = np.zeros((self.slabs, ky_n, 2, yl, 128), np.float32)
-        for s in range(self.slabs):
-            for k in range(ky_n):
-                near[s, k, 0] = cos[kept + k, s * yl : (s + 1) * yl, None]
-                near[s, k, 1] = sin[kept + k, s * yl : (s + 1) * yl, None]
-        return (
-            np.concatenate([high, high, low], axis=2),
-            np.stack(split_bf16(third[:, : (g - 1) * self.slabs * 8])),
-            final,
-        )
+            table[0, :, :, :, 2 * z], table[0, :, :, :, 2 * z + 1] = c, n
+            table[1, :, :, :, 2 * z], table[1, :, :, :, 2 * z + 1] = -n, c
+        early = table[:, :, : g - 1].reshape(2 * self.keep, (g - 1) * self.slabs * 8)
+        last = table[:, :, g - 1, 0, : self.rows].reshape(2 * self.keep, self.rows).T
+        last = np.broadcast_to(last[:, :, None], (*last.shape, 128))
+        return np.stack(split_bf16(early)), np.ascontiguousarray(last)
 
 
 def kernel(
-    plan, vel_hbm, vort_hbm, modes_hbm, second_hbm, third_hbm, final_hbm, out_ref,
+    plan, vel_hbm, vort_hbm, modes_hbm, third_hbm, final_hbm, out_ref,
     fields, modes, first, second, third, near, final, cross, quick, send, recv,
     field_sem, late_sem, send_sem, recv_sem,
 ):
@@ -239,10 +211,9 @@
         for c in range(3):
             pltpu.make_async_copy(source.at[c], fields.at[i, c], field_sem).start()
     late_loads = [
-        pltpu.make_async_copy(second_hbm.at[slab], second, late_sem.at[0]),
-        pltpu.make_async_copy(third_hbm, third, late_sem.at[1]),
-        pltpu.make_async_copy(modes_hbm, modes, late_sem.at[2]),
-        pltpu.make_async_copy(final_hbm, final, late_sem.at[3]),
+        pltpu.make_async_copy(third_hbm, third, late_sem.at[0]),
+        pltpu.make_async_copy(modes_hbm, modes, late_sem.at[1]),
+        pltpu.make_async_copy(final_hbm, final, late_sem.at[2]),
     ]
 
     barrier = pltpu.get_barrier_semaphore()
@@ -291,6 +262,18 @@
             start = k * plan.wide + s * 128
             for i in range(2):
                 first[i, 0:cells, start : start + 128] = table[i]
+    shape = (keep, 6 * plan.y_rows)
+    row = ramp(shape, 0)
+    wave = signed(row % plan.groups * plan.rows_ky + row // plan.groups).astype(jnp.float32)
+    line = ramp(shape, 1).astype(jnp.float32)
+    part = jnp.floor((line + 0.5) * (1.0 / plan.y_rows))
+    line = line - part * plan.y_rows
+    cosine, sine = turn(wave, line + (slab * plan.y_rows).astype(jnp.float32))
+    real = (part == 0) | (part == 2) | (part == 4)
+    for k, table in enumerate((jnp.where(real, cosine, sine), jnp.where(real, -sine, cosine))):
+        table_high = table.astype(jnp.bfloat16).astype(jnp.float32)
+        table = jnp.where(part < 4, table_high, table - table_high)
+        second[k * keep : (k + 1) * keep] = table.astype(jnp.bfloat16)
     if cells < 128:
         for i in range(2):
             first[i, cells:128] = jnp.zeros((128 - cells, first.shape[2]), jnp.bfloat16)
@@ -385,7 +368,6 @@
     along_x = mm(
         jnp.concatenate([high, low], axis=1), jnp.concatenate([first[0], first[0]], axis=0)
     ) + mm(high, first[1])
-    late_loads[0].wait()
     slot = lax.broadcasted_iota(jnp.int32, (area, 2 * plan.wide), 1) % 128 // plan.width
     along_x = [along_x[c * area : (c + 1) * area] for c in range(3)]
     along_x = jnp.where(slot == 0, along_x[0], jnp.where(slot == 1, along_x[1], along_x[2]))
@@ -443,7 +425,7 @@
     ksq = waves[0] * waves[0] + waves[1] * waves[1] + waves[2] * waves[2]
     inverse = 1.0 / jnp.maximum(ksq, 1.0)
     damp = (0.5 / (keep // 2) ** 2) * ksq
-    for load in late_loads[1:]:
+    for load in late_loads:
         load.wait()
     damped = [
         [
@@ -498,18 +480,18 @@
 
 def direct(plan, tables, velocity, vorticity, velocity_modes):
     modes = jnp.transpose(velocity_modes, (0, 2, 3, 4, 1))
-    second, third, final = tables
+    third, final = tables
     hbm = pl.BlockSpec(memory_space=pltpu.HBM)
     out = pl.pallas_call(
         functools.partial(kernel, plan),
         out_shape=pltpu.VMEM(modes.shape, jnp.float32),
-        in_specs=[hbm] * 6,
+        in_specs=[hbm] * 5,
         out_specs=pl.BlockSpec(memory_space=pltpu.VMEM),
         scratch_shapes=[
             pltpu.VMEM((2,) + velocity.shape, jnp.float32),
             pltpu.VMEM(modes.shape, jnp.float32),
             pltpu.VMEM((2, 128, 2 * plan.wide), jnp.bfloat16),
-            pltpu.VMEM(second.shape[1:], jnp.bfloat16),
+            pltpu.VMEM((2 * plan.keep, 6 * plan.y_rows), jnp.bfloat16),
             pltpu.VMEM(third.shape, jnp.bfloat16),
             pltpu.VMEM((plan.rows_ky, 2, plan.y_rows, 128), jnp.float32),
             pltpu.VMEM(final.shape, jnp.float32),
@@ -518,12 +500,12 @@
             pltpu.VMEM((plan.slabs * plan.groups * 8, 128), jnp.float32),
             pltpu.VMEM((plan.count, 8, 128), jnp.float32),
             pltpu.SemaphoreType.DMA,
-            pltpu.SemaphoreType.DMA((4,)),
+            pltpu.SemaphoreType.DMA((3,)),
             pltpu.SemaphoreType.DMA,
             pltpu.SemaphoreType.DMA((2,)),
         ],
         compiler_params=pltpu.CompilerParams(collective_id=0, has_side_effects=True),
-    )(velocity, vorticity, modes, second, third, final)
+    )(velocity, vorticity, modes, third, final)
     return jnp.transpose(out, (0, 4, 1, 2, 3))
 
 

time: 10.8 us -> 10.7 us (level)
  no operation moved by 1% of the time
where the time goes in v6:
time: 10.7 us; the launch traced here: 10.5 us
  Pallas kernels  9.83 us (92%)
  local copies, waits for them, and re-layouts  0.64 us (6%)
    pallas_call x1, Pallas kernels, direct(): pl.pallas_call(functools.partial(kernel, plan), out_shape=pltpu.VMEM(mode...  9.83 us
    unnamed x1, local copies, waits for them, and re-layouts  0.64 us

profile of v6, /device:TPU:0, one launch (start us, length us, event | category | flops | bytes accessed | tf_op | source)
XLA Modules:
  0.0 10.5 jit_solution(17517368845690630720)
XLA Ops:
  0.0 9.8 %shard_map.55 = f32[3,2,2,16,32]{4,3,2,1,0:T(8,128)S(1)} custom-call(f32[3,3,24,48]{3,2,1,0:T(8,128)} %vel_hbm.1, f32[3,3,24,48]{3,2,1,0:T(8,128)} %vort_hbm.1, f32[3,2,2,16,32]{4,3,2,1,0:T(8,128)} %bitcast.3, bf16[2,64,240]{2,1,0:T(8,128)(2,1)} %constant.4.clone.third_hbm, f32[6,64,128]{2,1,0:T(8,128)} %constant.5.clone.final_hbm), custom_call_target="tpu_custom_call" | custom-call | tf_op jit(solution)/shard_map/pallas_call | solution.py:485
  9.8 0.6 %copy.7 = f32[3,32,2,2,16]{1,4,3,2,0:T(8,128)} copy(f32[3,32,2,2,16]{1,4,3,2,0:T(8,128)S(1)} %bitcast.2) | data formatting | bytes 49152

commit v7 on v6

--- a/solution.py
+++ b/solution.py
@@ -279,8 +279,6 @@
             first[i, cells:128] = jnp.zeros((128 - cells, first.shape[2]), jnp.bfloat16)
 
     pltpu.make_async_copy(fields, fields, field_sem).wait()
-    for load in late_loads:
-        load.start()
     zl, yl = plan.z_rows, plan.y_rows
     area = zl * yl
     v, w = ([fields[i, c].reshape(area, cells) for c in range(3)] for i in range(2))
@@ -393,6 +391,9 @@
                 rows = pl.ds(s * plan.groups * 8 + 2 * z + k, plan.groups, stride=8)
                 send[rows, :] = total[:, s * 128 : (s + 1) * 128]
 
+    for load in late_loads:
+        load.start()
+
     @pl.when(jnp.logical_not(is_last))
     def _():
         open_with_near()

time: 10.7 us -> 10.7 us (level)
  no operation moved by 1% of the time
where the time goes in v7:
time: 10.7 us; the launch traced here: 10.5 us
  Pallas kernels  9.83 us (92%)
  local copies, waits for them, and re-layouts  0.64 us (6%)
    pallas_call x1, Pallas kernels, direct(): pl.pallas_call(functools.partial(kernel, plan), out_shape=pltpu.VMEM(mode...  9.83 us
    unnamed x1, local copies, waits for them, and re-layouts  0.64 us

profile of v7, /device:TPU:0, one launch (start us, length us, event | category | flops | bytes accessed | tf_op | source)
XLA Modules:
  0.0 10.5 jit_solution(3656755029355452815)
XLA Ops:
  0.0 9.8 %shard_map.55 = f32[3,2,2,16,32]{4,3,2,1,0:T(8,128)S(1)} custom-call(f32[3,3,24,48]{3,2,1,0:T(8,128)} %vel_hbm.1, f32[3,3,24,48]{3,2,1,0:T(8,128)} %vort_hbm.1, f32[3,2,2,16,32]{4,3,2,1,0:T(8,128)} %bitcast.3, bf16[2,64,240]{2,1,0:T(8,128)(2,1)} %constant.4.clone.third_hbm, f32[6,64,128]{2,1,0:T(8,128)} %constant.5.clone.final_hbm), custom_call_target="tpu_custom_call" | custom-call | tf_op jit(solution)/shard_map/pallas_call | solution.py:486
  9.8 0.6 %copy.7 = f32[3,32,2,2,16]{1,4,3,2,0:T(8,128)} copy(f32[3,32,2,2,16]{1,4,3,2,0:T(8,128)S(1)} %bitcast.2) | data formatting | bytes 49152

commit v8 on v7

--- a/solution.py
+++ b/solution.py
@@ -148,12 +148,18 @@
             return -1, 0, index
         return (far[spans.index(max(spans))], -sum(far), index) if far else (0, 0, index)
 
-    return sorted(every, key=key)
+    order = sorted(every, key=key)
+
+    def greeting(index):
+        far = sum(hops(index))
+        return order.index(index) >= len(order) // 2, far == 0, -far, index
+
+    return order, sorted(every, key=greeting)
 
 
 class Plan:
-    def __init__(self, mesh_shape, order, cells, keep, z_rows, y_rows):
-        self.order = order
+    def __init__(self, mesh_shape, orders, cells, keep, z_rows, y_rows):
+        self.order, self.greeted = orders
         self.cells, self.keep, self.z_rows, self.y_rows = cells, keep, z_rows, y_rows
         self.halves, self.pens, self.slabs = (mesh_shape[a] for a in AXES)
         self.groups = self.halves * self.pens
@@ -224,7 +230,7 @@
     def place(to):
         return (to[0] * plan.pens + to[1]) * plan.slabs + to[2]
 
-    for to in plan.order:
+    for to in plan.greeted:
 
         @pl.when(me != place(to))
         def _(to=to):
@@ -512,11 +518,11 @@
 
 def solution(mesh):
     sizes = dict(mesh.shape)
-    order = by_distance(mesh.devices)
+    orders = by_distance(mesh.devices)
 
     def run(velocity, vorticity, velocity_modes):
         _, z_rows, y_rows, cells = velocity.shape
-        plan = Plan(sizes, order, cells, velocity_modes.shape[1], z_rows, y_rows)
+        plan = Plan(sizes, orders, cells, velocity_modes.shape[1], z_rows, y_rows)
         if not plan.fits():
             return per_device(velocity, vorticity, velocity_modes)
         return direct(plan, plan.tables(), velocity, vorticity, velocity_modes)

time: 10.7 us -> 10.7 us (level)
  no operation moved by 1% of the time
where the time goes in v8:
time: 10.7 us; the launch traced here: 10.5 us
  Pallas kernels  9.82 us (92%)
  local copies, waits for them, and re-layouts  0.64 us (6%)
    pallas_call x1, Pallas kernels, direct(): pl.pallas_call(functools.partial(kernel, plan), out_shape=pltpu.VMEM(mode...  9.82 us
    unnamed x1, local copies, waits for them, and re-layouts  0.64 us

profile of v8, /device:TPU:0, one launch (start us, length us, event | category | flops | bytes accessed | tf_op | source)
XLA Modules:
  0.0 10.5 jit_solution(12357162012260466754)
XLA Ops:
  0.0 9.8 %shard_map.55 = f32[3,2,2,16,32]{4,3,2,1,0:T(8,128)S(1)} custom-call(f32[3,3,24,48]{3,2,1,0:T(8,128)} %vel_hbm.1, f32[3,3,24,48]{3,2,1,0:T(8,128)} %vort_hbm.1, f32[3,2,2,16,32]{4,3,2,1,0:T(8,128)} %bitcast.3, bf16[2,64,240]{2,1,0:T(8,128)(2,1)} %constant.4.clone.third_hbm, f32[6,64,128]{2,1,0:T(8,128)} %constant.5.clone.final_hbm), custom_call_target="tpu_custom_call" | custom-call | tf_op jit(solution)/shard_map/pallas_call | solution.py:492
  9.8 0.6 %copy.7 = f32[3,32,2,2,16]{1,4,3,2,0:T(8,128)} copy(f32[3,32,2,2,16]{1,4,3,2,0:T(8,128)S(1)} %bitcast.2) | data formatting | bytes 49152

commit v9 on v8

--- a/solution.py
+++ b/solution.py
@@ -215,7 +215,7 @@
     cells, keep = plan.cells, plan.keep
     for i, source in enumerate((vel_hbm, vort_hbm)):
         for c in range(3):
-            pltpu.make_async_copy(source.at[c], fields.at[i, c], field_sem).start()
+            pltpu.make_async_copy(source.at[c], fields.at[i, c], field_sem).start(priority=i)
     late_loads = [
         pltpu.make_async_copy(third_hbm, third, late_sem.at[0]),
         pltpu.make_async_copy(modes_hbm, modes, late_sem.at[1]),

time: 10.7 us -> 10.7 us (level)
  no operation moved by 1% of the time
where the time goes in v9:
time: 10.7 us; the launch traced here: 10.5 us
  Pallas kernels  9.82 us (92%)
  local copies, waits for them, and re-layouts  0.64 us (6%)
    pallas_call x1, Pallas kernels, direct(): pl.pallas_call(functools.partial(kernel, plan), out_shape=pltpu.VMEM(mode...  9.82 us
    unnamed x1, local copies, waits for them, and re-layouts  0.64 us

profile of v9, /device:TPU:0, one launch (start us, length us, event | category | flops | bytes accessed | tf_op | source)
XLA Modules:
  0.0 10.5 jit_solution(1100461331957382536)
XLA Ops:
  0.0 9.8 %shard_map.55 = f32[3,2,2,16,32]{4,3,2,1,0:T(8,128)S(1)} custom-call(f32[3,3,24,48]{3,2,1,0:T(8,128)} %vel_hbm.1, f32[3,3,24,48]{3,2,1,0:T(8,128)} %vort_hbm.1, f32[3,2,2,16,32]{4,3,2,1,0:T(8,128)} %bitcast.3, bf16[2,64,240]{2,1,0:T(8,128)(2,1)} %constant.4.clone.third_hbm, f32[6,64,128]{2,1,0:T(8,128)} %constant.5.clone.final_hbm), custom_call_target="tpu_custom_call" | custom-call | tf_op jit(solution)/shard_map/pallas_call | solution.py:492
  9.8 0.6 %copy.7 = f32[3,32,2,2,16]{1,4,3,2,0:T(8,128)} copy(f32[3,32,2,2,16]{1,4,3,2,0:T(8,128)S(1)} %bitcast.2) | data formatting | bytes 49152

commit v10 on v9

--- a/solution.py
+++ b/solution.py
@@ -398,7 +398,7 @@
                 send[rows, :] = total[:, s * 128 : (s + 1) * 128]
 
     for load in late_loads:
-        load.start()
+        load.start(priority=1)
 
     @pl.when(jnp.logical_not(is_last))
     def _():

time: 10.7 us -> 10.7 us (level)
  no operation moved by 1% of the time
where the time goes in v10:
time: 10.7 us; the launch traced here: 10.5 us
  Pallas kernels  9.82 us (92%)
  local copies, waits for them, and re-layouts  0.64 us (6%)
    pallas_call x1, Pallas kernels, direct(): pl.pallas_call(functools.partial(kernel, plan), out_shape=pltpu.VMEM(mode...  9.82 us
    unnamed x1, local copies, waits for them, and re-layouts  0.64 us

profile of v10, /device:TPU:0, one launch (start us, length us, event | category | flops | bytes accessed | tf_op | source)
XLA Modules:
  0.0 10.5 jit_solution(3369795305222415889)
XLA Ops:
  0.0 9.8 %shard_map.55 = f32[3,2,2,16,32]{4,3,2,1,0:T(8,128)S(1)} custom-call(f32[3,3,24,48]{3,2,1,0:T(8,128)} %vel_hbm.1, f32[3,3,24,48]{3,2,1,0:T(8,128)} %vort_hbm.1, f32[3,2,2,16,32]{4,3,2,1,0:T(8,128)} %bitcast.3, bf16[2,64,240]{2,1,0:T(8,128)(2,1)} %constant.4.clone.third_hbm, f32[6,64,128]{2,1,0:T(8,128)} %constant.5.clone.final_hbm), custom_call_target="tpu_custom_call" | custom-call | tf_op jit(solution)/shard_map/pallas_call | solution.py:492
  9.8 0.6 %copy.7 = f32[3,32,2,2,16]{1,4,3,2,0:T(8,128)} copy(f32[3,32,2,2,16]{1,4,3,2,0:T(8,128)S(1)} %bitcast.2) | data formatting | bytes 49152
